TPU v7x, 16 devices: a whole 2x2x2 slice. The times are simulated.
16 devices in a mesh: rep: 1, r: 2 (over z), s: 8 (over x, y, core).
Axes of the slice: x: 2, y: 2, z: 2, core: 2. Of those that a mesh axis runs over, the one named last changes fastest.
Arguments:
- x: bfloat16 [16, 2048, 896], P(('rep', 'r', 's'))
- dy: bfloat16 [16, 2048, 896], P(('rep', 'r', 's'))
- w_gate: bfloat16 [2, 896, 3584], P(None, 's')
- w_up: bfloat16 [2, 896, 3584], P(None, 's')
- w_down: bfloat16 [2, 3584, 896], P(None, 's')
- m_w_gate: float32 [2, 896, 3584], P(None, 's')
- m_w_up: float32 [2, 896, 3584], P(None, 's')
- m_w_down: float32 [2, 3584, 896], P(None, 's')
- v_w_gate: float32 [2, 896, 3584], P(None, 's')
- v_w_up: float32 [2, 896, 3584], P(None, 's')
- v_w_down: float32 [2, 3584, 896], P(None, 's')
Outputs:
- output 1: bfloat16 [2, 896, 3584], P('rep', 's')
- output 2: bfloat16 [2, 896, 3584], P('rep', 's')
- output 3: bfloat16 [2, 3584, 896], P('rep', 's')
- output 4: float32 [2, 896, 3584], P('rep', 's')
- output 5: float32 [2, 896, 3584], P('rep', 's')
- output 6: float32 [2, 3584, 896], P('rep', 's')
- output 7: float32 [2, 896, 3584], P('rep', 's')
- output 8: float32 [2, 896, 3584], P('rep', 's')
- output 9: float32 [2, 3584, 896], P('rep', 's')
All inputs are finite; a program needn't handle non-finite values.
Results may differ from a plain program's by a relative error of at most 0.022.
Values are sent between devices in bfloat16 or wider.
A program may use at most 2 GiB of HBM per device.

v0:
```python
import jax
import jax.numpy as jnp
from jax import lax
from jax.sharding import PartitionSpec as P

NAMES = ("w_gate", "w_up", "w_down")


def matmul(a, w):
    return jnp.dot(a, w, preferred_element_type=jnp.float32).astype(jnp.bfloat16)


def normed(h):
    wide = h.astype(jnp.float32)
    scale = lax.rsqrt(jnp.mean(wide**2, -1, keepdims=True) + 1e-6)
    return (wide * scale).astype(jnp.bfloat16)


def layer(h, w):
    a = normed(h)
    gate = jnp.dot(a, w["w_gate"], preferred_element_type=jnp.float32)
    up = jnp.dot(a, w["w_up"], preferred_element_type=jnp.float32)
    return h + matmul((jax.nn.silu(gate) * up).astype(jnp.bfloat16), w["w_down"])


def adamw(w, m, v, g):
    m = 0.9 * m + 0.1 * g
    v = 0.95 * v + 0.05 * g * g
    step = m * lax.rsqrt(v + 1e-8) + 0.1 * w
    return (w - 0.02 * step).astype(jnp.bfloat16), m, v


def clipped(gradients, sum_of_squares, count):
    factor = jnp.minimum(1.0, 0.5 * lax.rsqrt(sum_of_squares / count + 1e-30))
    return [g * factor for g in gradients]


def solution(mesh):
    def fetched(weights, number):
        return {name: lax.all_gather(w[number], "s", axis=0, tiled=True) for name, w in zip(NAMES, weights, strict=True)}

    def summed(term):
        return lax.psum(lax.psum_scatter(term, "s", scatter_dimension=0, tiled=True), "r")

    def step(x, dy, *arrays):
        weights, m, v = (arrays[i : i + 3] for i in (0, 3, 6))
        layers = weights[0].shape[0]
        h, kept = x[0], []
        for number in range(layers):
            kept.append(h)
            h = layer(h, fetched(weights, number))
        by_h, mine = dy[0], [None] * layers
        for number in reversed(range(layers)):
            _, back = jax.vjp(lambda w, h: layer(h, w), fetched(weights, number), kept[number])
            by_w, by_h = back(by_h)
            mine[number] = [summed(by_w[name]) for name in NAMES]
        gradients = [jnp.stack([mine[number][i] for number in range(layers)]).astype(jnp.float32) for i in range(3)]
        squares = lax.psum(sum(jnp.sum(g * g) for g in gradients), "s")
        gradients = clipped(gradients, squares, lax.psum(1, "s") * sum(g.size for g in gradients))
        new = [adamw(w.astype(jnp.float32), m, v, g) for w, m, v, g in zip(weights, m, v, gradients, strict=True)]
        return tuple(one[which] for which in range(3) for one in new)

    states, cut = P(("rep", "r", "s"), None, None), P(None, "s", None)
    return jax.shard_map(
        step,
        mesh=mesh,
        in_specs=(states, states) + (cut,) * 9,
        out_specs=(P("rep", "s", None),) * 9,
        check_vma=False,
    )
```

profile of v0, /device:TPU:0, one launch (start us, length us, event | category | flops | bytes accessed | tf_op | source)
XLA Modules:
  0.0 912.2 jit_solution(7793064235386811514)
XLA Ops:
  7.2 0.0 all-gather.13.cloned.1.call-start
  7.2 2.7 fusion.94
  10.0 0.0 all-gather.15.cloned.1.call-start
  10.1 2.6 fusion.93
  12.7 0.0 all-gather.17.cloned.1.call-start
  12.8 1.3 fusion.92
  14.1 0.0 all-gather.21.cloned.1.call-start
  14.1 0.5 all-gather.21.cloned.1.call-update
  14.7 0.0 all-gather.23.cloned.1.call-start
  14.7 0.5 all-gather.23.cloned.1.call-update
  15.2 0.0 all-gather.19.cloned.1.call-start
  15.3 0.5 all-gather.19.cloned.1.call-update
  15.8 0.0 reduce-scatter.15.cloned.1.call-start
  15.9 6.2 copy.20
  22.1 2.8 fusion.15
  24.9 6.1 copy.21
  31.0 24.2 %all-gather.13.cloned.1.call-done = bf16[1,896,3584]{2,1,0:T(8,128)(2,1)} async-done(((bf16[1,112,3584]{2,1,0:T(8,128)(2,1)}), bf16[1,896,3584]{2,1,0:T(8,128)(2,1)}) %all-gather.13.cloned.1.call-update) | async-done | bytes 6422544 | tf_op jit(solution)/shard_map/all_gather | solution.py:40
  55.2 24.1 %fusion.41 = f32[2048,3584]{1,0:T(8,128)} fusion(bf16[1,896,3584]{2,1,0:T(8,128)(2,1)} %all-gather.13.cloned.1.call-done, bf16[1,2048,896]{1,2,0:T(8,128)(2,1)} %copy.20, f32[2048]{0:T(1024)S(1)} %add_rsqrt_fusion), kind=kOutput, calls=%fused_computation.59 | convolution fusion | flops 13158842368 | bytes 39460864 | tf_op jit(solution)/shard_map/dot_general | solution.py:21
  79.3 20.3 %all-gather.15.cloned.1.call-done = bf16[1,896,3584]{2,1,0:T(8,128)(2,1)} async-done(((bf16[1,112,3584]{2,1,0:T(8,128)(2,1)}), bf16[1,896,3584]{2,1,0:T(8,128)(2,1)}) %all-gather.15.cloned.1.call-update) | async-done | bytes 6422544 | tf_op jit(solution)/shard_map/all_gather | solution.py:40
  99.5 33.8 %multiply_convert_fusion.1 = (bf16[2048,3584]{1,0:T(8,128)(2,1)}, f32[2048,3584]{1,0:T(8,128)}) fusion(f32[2048,3584]{1,0:T(8,128)} %fusion.41, bf16[1,896,3584]{2,1,0:T(8,128)(2,1)} %all-gather.15.cloned.1.call-done, bf16[1,2048,896]{1,2,0:T(8,128)(2,1)} %copy.20, f32[2048]{0:T(1024)S(1)} %add_rsqrt_fusion), kind=kOutput, calls=%fused_computation.17 | convolution fusion | flops 13202882560 | bytes 83501056 | tf_op jit(solution)/shard_map/dot_general | solution.py:22
  133.3 10.6 %all-gather.17.cloned.1.call-done = bf16[1,3584,896]{2,1,0:T(8,128)(2,1)} async-done(((bf16[1,448,896]{2,1,0:T(8,128)(2,1)}), bf16[1,3584,896]{2,1,0:T(8,128)(2,1)}) %all-gather.17.cloned.1.call-update) | async-done | bytes 6422544 | tf_op jit(solution)/shard_map/all_gather | solution.py:40
  143.9 21.1 %fusion.19 = (f32[2048]{0:T(1024)S(1)}, bf16[2048,896]{0,1:T(8,128)(2,1)}) fusion(bf16[2048,3584]{1,0:T(8,128)(2,1)} %get-tuple-element.30, bf16[1,3584,896]{2,1,0:T(8,128)(2,1)} %all-gather.17.cloned.1.call-done, bf16[1,2048,896]{1,2,0:T(8,128)(2,1)} %copy.20), kind=kOutput, calls=%fused_computation.37 | convolution fusion | flops 13162510336 | bytes 28450816 | tf_op jit(solution)/shard_map/dot_general | solution.py:10
  165.0 23.0 %all-gather.21.cloned.1.call-done = bf16[1,3584,896]{2,1,0:T(8,128)(2,1)} async-done(((bf16[1,448,896]{2,1,0:T(8,128)(2,1)}), bf16[1,3584,896]{2,1,0:T(8,128)(2,1)}) %all-gather.21.cloned.1.call-update) | async-done | bytes 6422544 | tf_op jit(solution)/shard_map/all_gather | solution.py:40
  188.1 22.1 %convolution_convert_fusion.1 = bf16[2048,3584]{1,0:T(8,128)(2,1)} fusion(bf16[1,3584,896]{2,1,0:T(8,128)(2,1)} %all-gather.21.cloned.1.call-done, bf16[1,2048,896]{2,1,0:T(8,128)(2,1)} %param.12), kind=kOutput, calls=%fused_computation.23 | convolution fusion | flops 13160677376 | bytes 24772608 | tf_op jit(solution)/shard_map/transpose(jvp())/dot_general | solution.py:10
  210.2 22.1 %all-gather.23.cloned.1.call-done = bf16[1,896,3584]{2,1,0:T(8,128)(2,1)} async-done(((bf16[1,112,3584]{2,1,0:T(8,128)(2,1)}), bf16[1,896,3584]{2,1,0:T(8,128)(2,1)}) %all-gather.23.cloned.1.call-update) | async-done | bytes 6422544 | tf_op jit(solution)/shard_map/all_gather | solution.py:40
  232.3 24.1 %fusion.28 = f32[2048,3584]{1,0:T(8,128)} fusion(bf16[1,896,3584]{2,1,0:T(8,128)(2,1)} %all-gather.23.cloned.1.call-done, bf16[2048,896]{0,1:T(8,128)(2,1)} %get-tuple-element.33, f32[2048]{0:T(1024)S(1)} %fusion.80), kind=kOutput, calls=%fused_computation.46 | convolution fusion | flops 13158842368 | bytes 39460864 | tf_op jit(solution)/shard_map/jvp()/dot_general | solution.py:22
  256.4 20.1 %all-gather.19.cloned.1.call-done = bf16[1,896,3584]{2,1,0:T(8,128)(2,1)} async-done(((bf16[1,112,3584]{2,1,0:T(8,128)(2,1)}), bf16[1,896,3584]{2,1,0:T(8,128)(2,1)}) %all-gather.19.cloned.1.call-update) | async-done | bytes 6422544 | tf_op jit(solution)/shard_map/all_gather | solution.py:40
  276.5 42.9 %fusion.2 = (bf16[2048,3584]{1,0:T(8,128)(2,1)}, f32[2048,3584]{1,0:T(8,128)}) fusion(f32[2048,3584]{1,0:T(8,128)} %fusion.28, bf16[2048,3584]{1,0:T(8,128)(2,1)} %convolution_convert_fusion.1, bf16[1,896,3584]{2,1,0:T(8,128)(2,1)} %all-gather.19.cloned.1.call-done, bf16[2048,896]{0,1:T(8,128)(2,1)} %get-tuple-element.33, f32[2048]{0:T(1024)S(1)} %fusion.80), kind=kOutput, calls=%fused_computation.8 | convolution fusion | flops 13246922752 | bytes 98181120 | tf_op jit(solution)/shard_map/jvp()/dot_general | solution.py:21
  319.4 22.7 %fusion.12 = bf16[2048,896]{0,1:T(8,128)(2,1)} fusion(bf16[2048,3584]{1,0:T(8,128)(2,1)} %convolution_convert_fusion.1, bf16[1,896,3584]{2,1,0:T(8,128)(2,1)} %all-gather.23.cloned.1.call-done, f32[2048,3584]{1,0:T(8,128)} %get-tuple-element.35), kind=kOutput, calls=%fused_computation.21 | convolution fusion | flops 13197377536 | bytes 54132736 | tf_op jit(solution)/shard_map/transpose(jvp())/dot_general | solution.py:22
  342.0 19.9 %fusion.21 = (f32[2048]{0:T(1024)S(1)}, bf16[2048,896]{0,1:T(8,128)(2,1)S(1)}) fusion(bf16[2048,896]{0,1:T(8,128)(2,1)S(1)} %copy-done.5, bf16[2048,896]{0,1:T(8,128)(2,1)} %fusion.12, bf16[2048,3584]{1,0:T(8,128)(2,1)} %get-tuple-element.34, bf16[1,896,3584]{2,1,0:T(8,128)(2,1)} %all-gather.19.cloned.1.call-done), kind=kOutput, calls=%fused_computation.39 | convolution fusion | flops 13162510336 | bytes 32120832 | tf_op jit(solution)/shard_map/transpose(jvp())/dot_general | solution.py:21
  362.0 3.0 fusion.47
  365.0 1.8 copy-done.6
  366.9 19.4 %convolution_convert_fusion.2 = bf16[3584,896]{1,0:T(8,128)(2,1)} fusion(bf16[2048,3584]{1,0:T(8,128)(2,1)} %get-tuple-element.30, bf16[2048,896]{0,1:T(8,128)(2,1)S(1)} %fusion.47), kind=kOutput, calls=%fused_computation.43 | convolution fusion | flops 13156548608 | bytes 24772608 | tf_op jit(solution)/shard_map/transpose(jvp())/dot_general | solution.py:10
  386.3 0.0 reduce-scatter.17.cloned.1.call-start
  386.3 26.8 %fusion.22 = bf16[3584,896]{1,0:T(8,128)(2,1)} fusion(f32[2048,3584]{1,0:T(8,128)} %fusion.28, bf16[1,2048,896]{2,1,0:T(8,128)(2,1)} %param.12, f32[2048,3584]{1,0:T(8,128)} %get-tuple-element.35), kind=kOutput, calls=%fused_computation.40 | convolution fusion | flops 13200588800 | bytes 68812800 | tf_op jit(solution)/shard_map/transpose(jvp())/dot_general | solution.py:10
  413.2 0.0 reduce-scatter.11.cloned.1.call-start
  413.2 22.0 %convolution_convert_fusion = bf16[2048,3584]{1,0:T(8,128)(2,1)} fusion(bf16[2048,896]{0,1:T(8,128)(2,1)} %copy-done.6, bf16[1,3584,896]{2,1,0:T(8,128)(2,1)} %all-gather.17.cloned.1.call-done), kind=kOutput, calls=%fused_computation.22 | convolution fusion | flops 13160677376 | bytes 24772608 | tf_op jit(solution)/shard_map/transpose(jvp())/dot_general | solution.py:10
  435.2 24.3 %fusion.24 = bf16[896,3584]{1,0:T(8,128)(2,1)} fusion(bf16[2048,3584]{1,0:T(8,128)(2,1)} %convolution_convert_fusion, f32[2048,3584]{1,0:T(8,128)} %fusion.41, bf16[1,2048,896]{1,2,0:T(8,128)(2,1)} %copy.20, f32[2048]{0:T(1024)S(1)} %copy-done.19), kind=kOutput, calls=%fused_computation.42 | convolution fusion | flops 13206093824 | bytes 54140928 | tf_op jit(solution)/shard_map/transpose(jvp())/dot_general | solution.py:22
  459.5 0.0 reduce-scatter.13.cloned.1.call-start
  459.6 0.6 copy-done.15
  460.2 24.0 %fusion.23 = bf16[896,3584]{1,0:T(8,128)(2,1)} fusion(bf16[2048,3584]{1,0:T(8,128)(2,1)} %convolution_convert_fusion.1, bf16[2048,896]{0,1:T(8,128)(2,1)} %get-tuple-element.33, f32[2048]{0:T(1024)S(1)} %copy-done.15, f32[2048,3584]{1,0:T(8,128)} %get-tuple-element.35), kind=kOutput, calls=%fused_computation.41 | convolution fusion | flops 13206093824 | bytes 54140928 | tf_op jit(solution)/shard_map/transpose(jvp())/dot_general | solution.py:22
  484.2 0.0 reduce-scatter.7.cloned.1.call-start
  484.3 33.4 %fusion.25 = bf16[896,3584]{1,0:T(8,128)(2,1)} fusion(f32[2048,3584]{1,0:T(8,128)} %fusion.41, f32[2048,3584]{1,0:T(8,128)} %get-tuple-element.31, bf16[2048,3584]{1,0:T(8,128)(2,1)} %convolution_convert_fusion, bf16[1,2048,896]{1,2,0:T(8,128)(2,1)} %copy.20, f32[2048]{0:T(1024)S(1)} %copy-done.19), kind=kOutput, calls=%fused_computation.45 | convolution fusion | flops 13242793984 | bytes 83501056 | tf_op jit(solution)/shard_map/transpose(jvp())/dot_general | solution.py:21
  517.7 0.0 reduce-scatter.9.cloned.1.call-start
  517.7 19.4 %convolution_convert_fusion.3 = bf16[896,3584]{1,0:T(8,128)(2,1)} fusion(bf16[2048,3584]{1,0:T(8,128)(2,1)} %get-tuple-element.34, bf16[2048,896]{0,1:T(8,128)(2,1)} %get-tuple-element.33, f32[2048]{0:T(1024)S(1)} %copy-done.15), kind=kOutput, calls=%fused_computation.44 | convolution fusion | flops 13158842368 | bytes 24780800 | tf_op jit(solution)/shard_map/transpose(jvp())/dot_general | solution.py:21
  537.2 0.0 all-reduce.3.cloned.1.call-start
  537.3 0.0 reduce-scatter.15.cloned.1.call-done
  537.3 24.4 %reduce-scatter.11.cloned.1.call-done = bf16[112,3584]{1,0:T(8,128)(2,1)} async-done(((bf16[896,3584]{1,0:T(8,128)(2,1)}), bf16[112,3584]{1,0:T(8,128)(2,1)}) %reduce-scatter.11.cloned.1.call-update) | async-done | bytes 802832 | tf_op jit(solution)/shard_map/reduce_scatter | solution.py:43
  561.7 59.4 %reduce-scatter.13.cloned.1.call-done = bf16[112,3584]{1,0:T(8,128)(2,1)} async-done(((bf16[896,3584]{1,0:T(8,128)(2,1)}), bf16[112,3584]{1,0:T(8,128)(2,1)}) %reduce-scatter.13.cloned.1.call-update) | async-done | bytes 802832 | tf_op jit(solution)/shard_map/reduce_scatter | solution.py:43
  621.0 59.5 %reduce-scatter.7.cloned.1.call-done = bf16[112,3584]{1,0:T(8,128)(2,1)} async-done(((bf16[896,3584]{1,0:T(8,128)(2,1)}), bf16[112,3584]{1,0:T(8,128)(2,1)}) %reduce-scatter.7.cloned.1.call-update) | async-done | bytes 802832 | tf_op jit(solution)/shard_map/reduce_scatter | solution.py:43
  680.6 59.4 %reduce-scatter.9.cloned.1.call-done = bf16[112,3584]{1,0:T(8,128)(2,1)} async-done(((bf16[896,3584]{1,0:T(8,128)(2,1)}), bf16[112,3584]{1,0:T(8,128)(2,1)}) %reduce-scatter.9.cloned.1.call-update) | async-done | bytes 802832 | tf_op jit(solution)/shard_map/reduce_scatter | solution.py:43
  740.0 120.6 %all-reduce.3.cloned.1.call-done = (bf16[1,112,3584]{2,1,0:T(8,128)(2,1)}, bf16[1,112,3584]{2,1,0:T(8,128)(2,1)}, bf16[1,112,3584]{2,1,0:T(8,128)(2,1)}, bf16[1,...) async-done(((bf16[1,112,3584]{2,1,0:T(8,128)(2,1)}, bf16[1,112,3584]{2,1,0:T(8,128)(2,1)}, bf16[1,112,3584]{2,1,0:T(8,128)(2,1)}, ...) | async-done | bytes 4816912 | tf_op jit(solution)/shard_map/psum | solution.py:43
  860.6 2.8 fusion.62
  863.4 2.8 fusion.61
  866.2 2.9 fusion.60
  871.0 14.0 %psum.55 = f32[]{:T(128)} all-reduce(f32[]{:T(128)S(6)} %add.111), channel_id=1, replica_groups=mesh['rep'=1,'r'=2,'s'=8] {'s'}, use_global_device_ids=true, to_apply=%region_18.19 | all-reduce | flops 1 | bytes 8 | tf_op jit(solution)/shard_map/psum | solution.py:58
  885.9 7.2 fusion.68
  893.1 0.2 copy-done.7
  893.3 1.5 copy-done.8
  894.8 0.9 copy-done.9
  895.7 0.9 copy-done.10
  896.6 0.1 copy-done.11
  896.8 0.2 copy-done.12
  897.0 8.5 fusion.59
  (46 shorter events, 0.3 us)
Async XLA Ops:
  7.2 5.6 copy-start.3
  7.2 48.0 %all-gather.13.cloned.1.call-start = ((), (), s32[]{:S(2)}) async-start(), calls=%async_computation.12 | async-start | bytes 7225344 | tf_op jit(solution)/shard_map/all_gather | solution.py:40
  10.0 89.5 %all-gather.15.cloned.1.call-start = ((), (), s32[]{:S(2)}) async-start(), calls=%async_computation.13 | async-start | bytes 7225344 | tf_op jit(solution)/shard_map/all_gather | solution.py:40
  12.7 131.2 %all-gather.17.cloned.1.call-start = ((), (), s32[]{:S(2)}) async-start(), calls=%async_computation.14 | async-start | bytes 7225344 | tf_op jit(solution)/shard_map/all_gather | solution.py:40
  14.1 174.0 %all-gather.21.cloned.1.call-start = ((), (), s32[]{:S(2)}) async-start(), calls=%async_computation.16 | async-start | bytes 7225344 | tf_op jit(solution)/shard_map/all_gather | solution.py:40
  14.7 217.6 %all-gather.23.cloned.1.call-start = ((), (), s32[]{:S(2)}) async-start(), calls=%async_computation.17 | async-start | bytes 7225344 | tf_op jit(solution)/shard_map/all_gather | solution.py:40
  15.2 261.2 %all-gather.19.cloned.1.call-start = ((), (), s32[]{:S(2)}) async-start(), calls=%async_computation.15 | async-start | bytes 7225344 | tf_op jit(solution)/shard_map/all_gather | solution.py:40
  15.8 521.5 %reduce-scatter.15.cloned.1.call-start = ((), (), s32[]{:S(2)}) async-start(), calls=%async_computation.10 | async-start | bytes 7225344 | tf_op jit(solution)/shard_map/reduce_scatter | solution.py:43
  24.9 74.6 %copy-start.18 = (f32[2048]{0:T(1024)}, f32[2048]{0:T(1024)S(1)}, u32[]{:S(2)}) copy-start(f32[2048]{0:T(1024)S(1)} %add_rsqrt_fusion) | copy-start | bytes 24580
  165.0 45.2 %copy-start.16 = (f32[2048]{0:T(1024)}, f32[2048]{0:T(1024)S(1)}, u32[]{:S(2)}) copy-start(f32[2048]{0:T(1024)S(1)} %get-tuple-element.32) | copy-start | bytes 24580
  165.0 196.9 %copy-start.14 = (f32[2048]{0:T(1024)}, f32[2048]{0:T(1024)S(1)}, u32[]{:S(2)}) copy-start(f32[2048]{0:T(1024)S(1)} %fusion.80) | copy-start | bytes 24580
  319.3 22.7 %copy-start.5 = (bf16[2048,896]{0,1:T(8,128)(2,1)S(1)}, bf16[2048,896]{0,1:T(8,128)(2,1)}, u32[]{:S(2)}) copy-start(bf16[2048,896]{0,1:T(8,128)(2,1)} %get-tuple-element.33) | copy-start | bytes 11010052
  342.0 19.9 %copy-start.17 = (f32[2048]{0:T(1024)S(1)}, f32[2048]{0:T(1024)}, u32[]{:S(2)}) copy-start(f32[2048]{0:T(1024)} %copy-done.16) | copy-start | bytes 24580
  342.0 20.0 %copy-start = (bf16[1,2048,896]{1,2,0:T(8,128)(2,1)S(1)}, bf16[1,2048,896]{1,2,0:T(8,128)(2,1)}, u32[]{:S(2)}) copy-start(bf16[1,2048,896]{1,2,0:T(8,128)(2,1)} %copy.21) | copy-start | bytes 11010052
  365.0 1.8 copy-start.6
  386.3 151.0 %reduce-scatter.17.cloned.1.call-start = ((), (), s32[]{:S(2)}) async-start(), calls=%async_computation.11 | async-start | bytes 7225344 | tf_op jit(solution)/shard_map/reduce_scatter | solution.py:43
  413.1 22.1 %copy-start.19 = (f32[2048]{0:T(1024)S(1)}, f32[2048]{0:T(1024)}, u32[]{:S(2)}) copy-start(f32[2048]{0:T(1024)} %copy-done.18) | copy-start | bytes 24580
  413.2 148.5 %reduce-scatter.11.cloned.1.call-start = ((), (), s32[]{:S(2)}) async-start(), calls=%async_computation.8 | async-start | bytes 7225344 | tf_op jit(solution)/shard_map/reduce_scatter | solution.py:43
  459.5 0.7 copy-start.15
  459.5 161.5 %reduce-scatter.13.cloned.1.call-start = ((), (), s32[]{:S(2)}) async-start(), calls=%async_computation.9 | async-start | bytes 7225344 | tf_op jit(solution)/shard_map/reduce_scatter | solution.py:43
  484.2 196.4 %reduce-scatter.7.cloned.1.call-start = ((), (), s32[]{:S(2)}) async-start(), calls=%async_computation.6 | async-start | bytes 7225344 | tf_op jit(solution)/shard_map/reduce_scatter | solution.py:43
  517.7 222.3 %reduce-scatter.9.cloned.1.call-start = ((), (), s32[]{:S(2)}) async-start(), calls=%async_computation.7 | async-start | bytes 7225344 | tf_op jit(solution)/shard_map/reduce_scatter | solution.py:43
  537.2 348.6 %copy-start.4 = (bf16[2,448,896]{2,1,0:T(8,128)(2,1)S(1)}, bf16[2,448,896]{2,1,0:T(8,128)(2,1)}, u32[]{:S(2)}) copy-start(bf16[2,448,896]{2,1,0:T(8,128)(2,1)} %param.15) | copy-start | bytes 4816900
  537.2 323.4 %all-reduce.3.cloned.1.call-start = ((), (), s32[]{:S(2)}) async-start(), calls=%async_computation.18 | async-start | bytes 9633792 | tf_op jit(solution)/shard_map/psum | solution.py:43
  866.2 26.9 %copy-start.13 = (bf16[1,112,3584]{2,1,0:T(8,128)(2,1)S(1)}, bf16[1,112,3584]{2,1,0:T(8,128)(2,1)}, u32[]{:S(2)}) copy-start(bf16[1,112,3584]{2,1,0:T(8,128)(2,1)} %get-tuple-element.11) | copy-start | bytes 2408452
  885.8 7.3 copy-start.1
  885.8 7.3 copy-start.2
  885.8 7.5 copy-start.7
  885.8 9.0 copy-start.8
  885.8 9.9 %copy-start.9 = (f32[2,112,3584]{2,1,0:T(8,128)S(1)}, f32[2,112,3584]{2,1,0:T(8,128)}, u32[]{:S(2)}) copy-start(f32[2,112,3584]{2,1,0:T(8,128)} %param.20) | copy-start | bytes 9633796
  885.8 10.8 %copy-start.10 = (f32[2,112,3584]{2,1,0:T(8,128)S(1)}, f32[2,112,3584]{2,1,0:T(8,128)}, u32[]{:S(2)}) copy-start(f32[2,112,3584]{2,1,0:T(8,128)} %param.17) | copy-start | bytes 9633796
  885.8 10.9 %copy-start.11 = (bf16[1,112,3584]{2,1,0:T(8,128)(2,1)S(1)}, bf16[1,112,3584]{2,1,0:T(8,128)(2,1)}, u32[]{:S(2)}) copy-start(bf16[1,112,3584]{2,1,0:T(8,128)(2,1)} %get-tuple-element.9) | copy-start | bytes 2408452
  885.9 11.1 %copy-start.12 = (bf16[1,112,3584]{2,1,0:T(8,128)(2,1)S(1)}, bf16[1,112,3584]{2,1,0:T(8,128)(2,1)}, u32[]{:S(2)}) copy-start(bf16[1,112,3584]{2,1,0:T(8,128)(2,1)} %get-tuple-element.10) | copy-start | bytes 2408452
Sparse Core Ops, SparseCore 0:
  10.4 44.7 all-gather.12
  57.6 41.8 all-gather.14
  101.9 41.8 all-gather.16
  146.1 41.8 all-gather.20
  190.3 41.8 all-gather.22
  234.6 41.8 all-gather.18
  386.4 56.1 reduce-scatter.14
  445.9 56.1 reduce-scatter.16
  505.5 56.1 reduce-scatter.10
  564.9 56.1 reduce-scatter.12
  624.4 56.1 reduce-scatter.6
  683.8 56.1 reduce-scatter.8
  743.1 117.4 all-reduce.2
where the time goes:
time: 920 us; the launch traced here: 912 us
  waiting for transfers between devices  445 us (48%)
  matrix products  380 us (41%)
  other arithmetic  30 us (3%)
  local copies, waits for them, and re-layouts  25.4 us (3%)
  between operations  17 us (2%)
  blocking collectives  14 us (2%)
    reduce_scatter x6, waiting for transfers between devices, summed(): lax.psum_scatter(term, 's', scatter_dimension=0, tiled=True)  203 us
    dot_general x5, matrix products, layer(): gate = jnp.dot(a, w['w_gate'], preferred_element_type=jnp.float32)  140 us
    dot_general x5, matrix products, layer(): up = jnp.dot(a, w['w_up'], preferred_element_type=jnp.float32)  129 us
    psum x1, waiting for transfers between devices, summed(): lax.psum(lax.psum_scatter(term, 's', scatter_dimension=0, tiled=True), 'r')  121 us
    all_gather x6, waiting for transfers between devices, fetched(): lax.all_gather(w[number], 's', axis=0, tiled=True)  120 us
    dot_general x5, matrix products, matmul(): jnp.dot(a, w, preferred_element_type=jnp.float32).astype(jnp.bfloat16)  111 us
    unnamed x42, local copies, waits for them, and re-layouts  18.7 us
  transfers between devices with their start and end apart: 13, of which 11 were waited for; matrix products, arithmetic and copies ran while one was open for 32% of the time, Pallas kernels for 0%

commit v1 on v0

v1 whole, which is shorter than its diff:
```python
import jax
import jax.numpy as jnp
from jax import lax
from jax.experimental import pallas as pl
from jax.experimental.pallas import tpu as pltpu
from jax.sharding import PartitionSpec as P

MESH = pl.DeviceIdType.MESH
T, D, FF = 2048, 896, 3584
TILES, WIDE, ROWS = 7, 512, 512
BLOCKS = T // ROWS
STEPS = 2 * TILES
F32, BF16 = jnp.float32, jnp.bfloat16
VMEM_LIMIT = 67_043_328
ANY = pl.BlockSpec(memory_space=pl.ANY)


def dot(a, b, contract=(1, 0)):
    return lax.dot_general(a, b, (((contract[0],), (contract[1],)), ((), ())), preferred_element_type=F32)


def normed(h):
    wide = h.astype(F32)
    scale = lax.rsqrt(jnp.mean(wide**2, -1, keepdims=True) + 1e-6)
    return (wide * scale).astype(BF16)


def block(i):
    return pl.ds(pl.multiple_of(i * ROWS, ROWS), ROWS)


class Place:
    def __init__(self):
        r, s = lax.axis_index("r"), lax.axis_index("s")
        c, q = s % 2, s // 2
        y, x = q % 2, q // 2
        self.r, self.s, self.c, self.q = r, s, c, q
        dx, dy = 2 - 4 * x, 1 - 2 * y
        self.qx, self.qy, self.qd = q + dx, q + dy, q + dx + dy
        self.sx, self.sy, self.sc = s + 2 * dx, s + 2 * dy, s + 1 - 2 * c
        self.sd = s + 2 * dx + 2 * dy
        self.sa = self.sx + r * (self.sy - self.sx)
        self.sb = self.sy + r * (self.sx - self.sy)
        self.to_a, self.to_b = {"s": self.sa}, {"s": self.sb}
        self.to_x, self.to_y, self.to_c, self.to_z = {"s": self.sx}, {"s": self.sy}, {"s": self.sc}, {"r": 1 - r}


def barrier(at):
    sem = pltpu.get_barrier_semaphore()
    for to in (at.to_x, at.to_y, at.to_c, at.to_z):
        pl.semaphore_signal(sem, inc=1, device_id=to, device_id_type=MESH)
    pl.semaphore_wait(sem, 4)


class Gather:
    def __init__(self, at, piece, send, recv):
        self.at, self.piece, self.send, self.recv = at, piece, send, recv

    def copy(self, way, n, shard, to):
        ref = self.piece(n, shard)
        return pltpu.make_async_remote_copy(
            src_ref=ref, dst_ref=ref, send_sem=self.send.at[way, n], recv_sem=self.recv.at[way, n], device_id=to, device_id_type=MESH
        )

    def own(self, n):
        self.copy(0, n, self.at.s, self.at.to_a).start()
        self.copy(3, n, self.at.s, self.at.to_c).start()

    def first(self, n):
        at = self.at
        self.copy(0, n, at.sa, at.to_a).wait_recv()
        self.copy(1, n, at.sa, at.to_z).start()
        self.copy(2, n, at.sa, at.to_b).start()
        self.copy(4, n, at.sa, at.to_c).start()

    def second(self, n):
        at = self.at
        self.copy(1, n, at.sb, at.to_z).wait_recv()
        self.copy(5, n, at.sb, at.to_c).start()
        self.copy(2, n, at.sd, at.to_b).wait_recv()
        self.copy(6, n, at.sd, at.to_c).start()

    def whole(self, n):
        at = self.at
        across = at.sc - at.s
        for way, shard in ((3, at.s), (4, at.sa), (5, at.sb), (6, at.sd)):
            self.copy(way, n, shard + across, at.to_c).wait_recv()

    def sent(self, n):
        at = self.at
        for way, shard, to in (
            (0, at.s, at.to_a), (1, at.sa, at.to_z), (2, at.sa, at.to_b),
            (3, at.s, at.to_c), (4, at.sa, at.to_c), (5, at.sb, at.to_c), (6, at.sd, at.to_c),
        ):
            self.copy(way, n, shard, to).wait_send()


def load_own(at, layer, wg_h, wu_h, wd_h, WGU, WD, own):
    for i in range(TILES):
        for which, w in enumerate((wg_h, wu_h)):
            for k in range(4):
                pltpu.make_async_copy(
                    w.at[layer, :, pl.ds(k * 896 + i * 128, 128)], WGU.at[i, which, at.s, :, pl.ds(k * 128, 128)], own.at[i]
                ).start()
    pltpu.make_async_copy(wd_h.at[layer], WD.at[at.q, pl.ds(at.c * 7, 7)], own.at[TILES]).start()


def wait_own_tile(at, i, WGU, own):
    pltpu.make_async_copy(WGU.at[i, :, at.s], WGU.at[i, :, at.s], own.at[i]).wait()


def wait_own_down(at, wd_h, layer, WD, own):
    pltpu.make_async_copy(wd_h.at[layer], WD.at[at.q, pl.ds(at.c * 7, 7)], own.at[TILES]).wait()


def gathers(at, WGU, WD, sgu, rgu, sd, rd):
    gu = Gather(at, lambda n, s: WGU.at[n, :, s], sgu, rgu)
    down = Gather(at, lambda n, s: WD.at[s // 2, (s % 2) * 7 + n], sd, rd)
    return gu, down


def gate_up(WGU, i, which):
    return WGU[i, which].reshape(D, WIDE)


def down_tile(WD, i):
    return WD[:, pl.ds(2 * i, 2)].reshape(WIDE, D)


def forward_kernel(
    x_h, wg_h, wu_h, wd_h,
    gu_o, a0t_o, h1_o, a1_o, a1t_o, wd_o,
    WGU, WD, X, A, AT, MID, ST,
    load, own, stage, out, sgu, rgu, sd, rd,
):
    at = Place()
    load_own(at, 0, wg_h, wu_h, wd_h, WGU, WD, own)
    x_in = pltpu.make_async_copy(x_h, X, load)
    x_in.start()
    barrier(at)
    gu, down = gathers(at, WGU, WD, sgu, rgu, sd, rd)

    def start_tile(n, _):
        wait_own_tile(at, n, WGU, own)
        gu.own(n)
        return 0

    lax.fori_loop(0, TILES, start_tile, 0)
    wait_own_down(at, wd_h, 0, WD, own)
    lax.fori_loop(0, TILES, lambda n, _: (down.own(n), 0)[1], 0)
    x_in.wait()

    def norm(m, _):
        a = normed(X[block(m), :])
        A[block(m), :] = a
        AT[:, :, block(m)] = a.T.reshape(2, 448, ROWS)
        return 0

    lax.fori_loop(0, BLOCKS, norm, 0)
    a0t_out = pltpu.make_async_copy(AT, a0t_o, out.at[0])
    a0t_out.start()
    gu.first(0)

    def staged(i, m, slot):
        return pltpu.make_async_copy(ST.at[slot], gu_o.at[i, :, block(m), :], stage.at[slot])

    def tile(i, _):
        pl.when(i < TILES - 1)(lambda: gu.first(i + 1))
        gu.second(i)
        gu.whole(i)

        def rows(m, _):
            slot = m % 2
            pl.when(i * BLOCKS + m >= 2)(lambda: staged(i, m, slot).wait())
            a = A[block(m), :]
            gate = dot(a, gate_up(WGU, i, 0))
            up = dot(a, gate_up(WGU, i, 1))
            ST[slot, 0] = gate
            ST[slot, 1] = up
            staged(i, m, slot).start()
            MID[i, block(m), :] = (gate * jax.nn.sigmoid(gate) * up).astype(BF16)
            return 0

        return lax.fori_loop(0, BLOCKS, rows, 0)

    lax.fori_loop(0, TILES, tile, 0)
    down.first(0)

    def piece(n, _):
        pl.when(n < TILES - 1)(lambda: down.first(n + 1))
        down.second(n)
        down.whole(n)
        return 0

    lax.fori_loop(0, TILES, piece, 0)
    wd_out = pltpu.make_async_copy(WD, wd_o, out.at[1])
    wd_out.start()
    a0t_out.wait()

    def finish(m, _):
        total = dot(MID[0, block(m), :], down_tile(WD, 0))
        for i in range(1, TILES):
            total += dot(MID[i, block(m), :], down_tile(WD, i))
        h = (X[block(m), :].astype(F32) + total.astype(BF16).astype(F32)).astype(BF16)
        X[block(m), :] = h
        a = normed(h)
        A[block(m), :] = a
        AT[:, :, block(m)] = a.T.reshape(2, 448, ROWS)
        return 0

    lax.fori_loop(0, BLOCKS, finish, 0)
    outs = [pltpu.make_async_copy(v, o, out.at[2 + k]) for k, (v, o) in enumerate(((X, h1_o), (A, a1_o), (AT, a1t_o)))]
    for o in outs:
        o.start()
    for slot in range(2):
        staged(TILES - 1, slot, slot).wait()

    def sent(n, _):
        gu.sent(n)
        down.sent(n)
        return 0

    lax.fori_loop(0, TILES, sent, 0)
    wd_out.wait()
    for o in outs:
        o.wait()


def added(a, b):
    return (a.astype(F32) + b.astype(F32)).astype(BF16)


def backward_kernel(
    a1_h, a1t_h, h1_h, dy_h, a0t_h, gu_h, wd0_h, wg_h, wu_h, wd_h,
    gg_o, gu_o, gd_o, sqw_o, sqd_o,
    WGU, WD, A, AT, DY, ACC, MID, DG, DU, TW, TD, RW, RD, FW, FD, BW, BD, ZW, ZD, OW, OD,
    load, own, gus, sgu, rgu, sd, rd, pair_s, pair_r, first_s, first_r, second_s, second_r, z_s, z_r, ow_s, od_s, od_remote_s, od_r,
    pair_free, first_x, first_y, second_x, second_y, z_free,
):
    at = Place()
    c, q, qx, qy, qd = at.c, at.q, at.qx, at.qy, at.qd
    load_own(at, 1, wg_h, wu_h, wd_h, WGU, WD, own)
    loads = [pltpu.make_async_copy(h, v, load.at[k]) for k, (h, v) in enumerate(((a1_h, A), (a1t_h, AT), (dy_h, DY)))]
    for one in loads:
        one.start()
    h1_in = pltpu.make_async_copy(h1_h, A, load.at[0])
    wd0_in = pltpu.make_async_copy(wd0_h, WD, load.at[2])
    a0t_in = pltpu.make_async_copy(a0t_h, AT, load.at[1])
    barrier(at)
    gather, down = gathers(at, WGU, WD, sgu, rgu, sd, rd)
    wait_own_down(at, wd_h, 1, WD, own)
    lax.fori_loop(0, TILES, lambda n, _: (down.own(n), 0)[1], 0)

    def start_tile(n, _):
        wait_own_tile(at, n, WGU, own)
        gather.own(n)
        return 0

    lax.fori_loop(0, TILES, start_tile, 0)
    sqw_o[...] = jnp.zeros_like(sqw_o)
    sqd_o[...] = jnp.zeros_like(sqd_o)
    down.first(0)

    def piece(n, _):
        pl.when(n < TILES - 1)(lambda: down.first(n + 1))
        down.second(n)
        return 0

    lax.fori_loop(0, TILES, piece, 0)
    gather.first(0)
    lax.fori_loop(0, TILES, lambda n, _: (down.whole(n), 0)[1], 0)
    gather.second(0)
    for one in loads:
        one.wait()

    def remote(src, dst, send, recv, to):
        return pltpu.make_async_remote_copy(src_ref=src, dst_ref=dst, send_sem=send, recv_sem=recv, device_id=to, device_id_type=MESH)

    def credit(sem, to):
        pl.semaphore_signal(sem, inc=1, device_id=to, device_id_type=MESH)

    def pair_copies(t):
        k, j = t % 3, t % 2
        return [
            remote(TW.at[k, :, :, 1 - c], RW.at[j], pair_s.at[0, j], pair_r.at[0, j], at.to_c),
            remote(TD.at[k, :, 1 - c], RD.at[j], pair_s.at[1, j], pair_r.at[1, j], at.to_c),
        ]

    def pair_send(t):
        pl.when(t >= 2)(lambda: pl.semaphore_wait(pair_free, 1))
        for one in pair_copies(t):
            one.start()

    def pair_add(t):
        k, j = t % 3, t % 2
        for one in pair_copies(t):
            one.wait()

        def chip(p, _):
            for which in range(2):
                TW[k, which, p, c] = added(TW[k, which, p, c], RW[j, which, p])
            TD[k, p, c] = added(TD[k, p, c], RD[j, p])
            return 0

        lax.fori_loop(0, 4, chip, 0)
        pl.when(t < STEPS - 2)(lambda: credit(pair_free, at.to_c))

    def ways(t):
        turn = t % 2
        x, y = (at.sx, qx), (at.sy, qy)
        mixed = tuple(a + turn * (b - a) for a, b in zip(x, y))
        other = tuple(b + turn * (a - b) for a, b in zip(x, y))
        return (x, y), (y, x), (mixed, other)

    def buffers(t, which):
        k, j = t % 3, t % 2
        if which < 2:
            return (lambda p: TW.at[k, which, p, c]), (lambda n: FW.at[j, which, n]), BW.at[j, which]
        return (lambda p: TD.at[k, p, c]), (lambda n: FD.at[j, n]), BD.at[j]

    def first_copies(t):
        j, copies = t % 2, []
        for which, (one, _) in enumerate(ways(t)):
            mine, into, _ = buffers(t, which)
            for n, p in enumerate((one[1], qd)):
                copies.append(remote(mine(p), into(n), first_s.at[2 * which + n, j], first_r.at[2 * which + n, j], {"s": one[0]}))
        return copies

    def first_send(t):
        @pl.when(t >= 2)
        def _():
            pl.semaphore_wait(first_x, 1)
            pl.semaphore_wait(first_y, 1)

        for one in first_copies(t):
            one.start()

    def first_add(t):
        for one in first_copies(t):
            one.wait()
        for which, (_, two) in enumerate(ways(t)):
            mine, into, _ = buffers(t, which)
            for n, p in enumerate((q, two[1])):
                mine(p)[...] = added(mine(p)[...], into(n)[...])

        @pl.when(t < STEPS - 2)
        def _():
            credit(first_x, at.to_x)
            credit(first_y, at.to_y)

    def second_copies(t):
        j, copies = t % 2, []
        for which, (_, two) in enumerate(ways(t)):
            mine, _, into = buffers(t, which)
            copies.append(remote(mine(two[1]), into, second_s.at[which, j], second_r.at[which, j], {"s": two[0]}))
        return copies

    def second_send(t):
        @pl.when(t >= 2)
        def _():
            pl.semaphore_wait(second_x, 1)
            pl.semaphore_wait(second_y, 1)

        for one in second_copies(t):
            one.start()

    def second_add(t):
        for one in second_copies(t):
            one.wait()
        for which in range(3):
            mine, _, into = buffers(t, which)
            mine(q)[...] = added(mine(q)[...], into[...])

        @pl.when(t < STEPS - 2)
        def _():
            credit(second_x, at.to_x)
            credit(second_y, at.to_y)

    def z_copies(t):
        k, j = t % 3, t % 2
        return [
            remote(TW.at[k, :, q, c], ZW.at[j], z_s.at[0, j], z_r.at[0, j], at.to_z),
            remote(TD.at[k, q, c], ZD.at[j], z_s.at[1, j], z_r.at[1, j], at.to_z),
        ]

    def z_send(t):
        pl.when(t >= 2)(lambda: pl.semaphore_wait(z_free, 1))
        for one in z_copies(t):
            one.start()

    def half(t, core):
        number = (t % TILES) * 2 + core
        return number // 7, number % 7

    def layer_of(t):
        return 1 - t // TILES

    def wide_out(t):
        j, i = t % 2, t % TILES
        for which, o in enumerate((gg_o, gu_o)):
            for k in range(4):
                lanes = pl.ds(pl.multiple_of(k * 896 + i * 128, 128), 128)
                yield pltpu.make_async_copy(OW.at[j, which, :, pl.ds(k * 128, 128)], o.at[layer_of(t), :, lanes], ow_s.at[j])

    def down_local(t):
        _, number = half(t, c)
        return pltpu.make_async_copy(OD.at[t % 2], gd_o.at[layer_of(t), number], od_s.at[t % 2])

    def down_remote(t, core):
        _, number = half(t, core)
        return remote(OD.at[t % 2], gd_o.at[layer_of(t), number], od_remote_s.at[t % 2], od_r.at[t], at.to_c)

    def out_start(t):
        for one in wide_out(t):
            one.start()
        owner, _ = half(t, c)
        pl.when(owner == c)(lambda: down_local(t).start())
        pl.when(owner != c)(lambda: down_remote(t, c).start())

    def out_wait(t):
        j = t % 2
        pltpu.make_async_copy(OW.at[j], OW.at[j], ow_s.at[j]).wait()
        owner, _ = half(t, c)
        pl.when(owner == c)(lambda: down_local(t).wait())
        pl.when(owner != c)(lambda: down_remote(t, c).wait_send())

    def z_add(t):
        k, j = t % 3, t % 2
        pl.when(t >= 2)(lambda: out_wait(t - 2))
        for one in z_copies(t):
            one.wait()
        for which in range(2):
            g = added(TW[k, which, q, c], ZW[j, which])
            OW[j, which] = g
            wide = g.astype(F32)
            sqw_o[...] += jnp.sum(wide * wide, 0, keepdims=True)
        g = added(TD[k, q, c], ZD[j])
        OD[j] = g
        wide = g.astype(F32)
        sqd_o[...] += jnp.sum(wide * wide, 0, keepdims=True)
        pl.when(t < STEPS - 2)(lambda: credit(z_free, at.to_z))
        out_start(t)

    def between(gate, up, by_mid):
        sig = jax.nn.sigmoid(gate)
        silu = gate * sig
        by_gate = by_mid * up * (sig + silu * (1.0 - sig))
        return (silu * up).astype(BF16), by_gate.astype(BF16), (by_mid * silu).astype(BF16)

    def store_between(m, values):
        for ref, value in zip((MID, DG, DU), values):
            ref[block(m), :] = value

    def layer_one(i):
        gather.whole(i)
        pl.when(i < TILES - 1)(lambda: gather.first(i + 1))

        @pl.when(i == 0)
        def _():
            ACC[...] = jnp.zeros_like(ACC)

        def rows(m, _):
            a = A[block(m), :]
            gate = dot(a, gate_up(WGU, i, 0))
            up = dot(a, gate_up(WGU, i, 1))
            by_mid = dot(DY[block(m), :], down_tile(WD, i), (1, 1)).astype(BF16).astype(F32)
            values = between(gate, up, by_mid)
            store_between(m, values)
            ACC[block(m), :] += dot(values[1], gate_up(WGU, i, 0), (1, 1)) + dot(values[2], gate_up(WGU, i, 1), (1, 1))
            return 0

        lax.fori_loop(0, BLOCKS, rows, 0)

    def kept(n):
        i, m, slot = n // BLOCKS, n % BLOCKS, n % 2
        return [
            pltpu.make_async_copy(
                gu_h.at[i, which, block(m), :], ACC.at[pl.ds(pl.multiple_of(slot * 1024 + which * 512, 512), 512), pl.ds(0, 512)], gus.at[slot, which]
            )
            for which in range(2)
        ]

    def turn():
        a0t_in.start()
        h1_in.wait()
        wd0_in.wait()

        def rows(m, _):
            wide = A[block(m), :].astype(F32)
            by_a = ACC[block(m), :].astype(BF16).astype(F32)
            scale = lax.rsqrt(jnp.mean(wide**2, -1, keepdims=True) + 1e-6)
            along = jnp.mean(by_a * wide, -1, keepdims=True) * scale * scale
            by_h = (scale * (by_a - wide * along)).astype(BF16)
            DY[block(m), :] = added(DY[block(m), :], by_h)
            return 0

        lax.fori_loop(0, BLOCKS, rows, 0)
        for one in kept(0):
            one.start()
        a0t_in.wait()

    def layer_zero(i):
        def rows(m, _):
            n = i * BLOCKS + m
            slot = n % 2

            @pl.when(n + 1 < TILES * BLOCKS)
            def _():
                for one in kept(n + 1):
                    one.start()

            for one in kept(n):
                one.wait()
            gate, up = (ACC[pl.ds(pl.multiple_of(slot * 1024 + which * 512, 512), 512), pl.ds(0, 512)] for which in range(2))
            by_mid = dot(DY[block(m), :], down_tile(WD, i), (1, 1)).astype(BF16).astype(F32)
            store_between(m, between(gate, up, by_mid))
            return 0

        lax.fori_loop(0, BLOCKS, rows, 0)

    def gradients(t):
        k = t % 3

        def rows(half, _):
            for which, by in enumerate((DG, DU)):
                TW[k, which, pl.ds(2 * half, 2)] = dot(AT[half], by[...]).astype(BF16).reshape(2, 2, 112, WIDE)
            return 0

        lax.fori_loop(0, 2, rows, 0)
        TD[k] = dot(MID[...], DY[...], (0, 0)).astype(BF16).reshape(4, 2, 64, D)

    def step(t, _):
        pl.when(t < TILES)(lambda: layer_one(t))
        pl.when(t == TILES)(turn)
        pl.when((t >= TILES) & (t < STEPS))(lambda: layer_zero(t - TILES))

        pl.when(t < TILES - 1)(lambda: gather.second(t + 1))

        @pl.when(t == TILES - 1)
        def _():
            h1_in.start()
            lax.fori_loop(0, TILES, lambda n, _: (down.sent(n), 0)[1], 0)
            wd0_in.start()

        @pl.when((t >= 1) & (t <= STEPS))
        def _():
            pair_add(t - 1)
            first_send(t - 1)

        @pl.when(t >= 2)
        def _():
            second_add(t - 2)
            z_send(t - 2)

        @pl.when(t < STEPS)
        def _():
            gradients(t)
            pair_send(t)

        @pl.when((t >= 1) & (t <= STEPS))
        def _():
            first_add(t - 1)
            second_send(t - 1)

        pl.when(t >= 2)(lambda: z_add(t - 2))
        return 0

    lax.fori_loop(0, STEPS + 2, step, 0)
    out_wait(STEPS - 2)
    out_wait(STEPS - 1)

    lax.fori_loop(0, TILES, lambda n, _: (gather.sent(n), 0)[1], 0)

    def arrived(t, _):
        owner, _ = half(t, 1 - c)
        pl.when(owner == c)(lambda: down_remote(t, 1 - c).wait_recv())
        return 0

    lax.fori_loop(0, STEPS, arrived, 0)


def shape(dims, dtype=BF16):
    return jax.ShapeDtypeStruct(dims, dtype)


def sems(*dims):
    return pltpu.SemaphoreType.DMA(dims)


GATHER_SEMS = [sems(7, TILES)] * 4


def forward(x, w_gate, w_up, w_down):
    return pl.pallas_call(
        forward_kernel,
        name="forward",
        out_shape=[
            shape((TILES, 2, T, WIDE), F32), shape((2, 448, T)), shape((T, D)), shape((T, D)), shape((2, 448, T)), shape((4, 14, 64, D)),
        ],
        in_specs=[ANY] * 4,
        out_specs=[ANY] * 6,
        scratch_shapes=[
            pltpu.VMEM((TILES, 2, 8, 112, WIDE), BF16), pltpu.VMEM((4, 14, 64, D), BF16), pltpu.VMEM((T, D), BF16), pltpu.VMEM((T, D), BF16),
            pltpu.VMEM((2, 448, T), BF16), pltpu.VMEM((TILES, T, WIDE), BF16), pltpu.VMEM((2, 2, ROWS, WIDE), F32),
            pltpu.SemaphoreType.DMA, sems(TILES + 1), sems(2), sems(5), *GATHER_SEMS,
        ],
        compiler_params=pltpu.CompilerParams(collective_id=0, has_side_effects=True, vmem_limit_bytes=VMEM_LIMIT),
    )(x, w_gate, w_up, w_down)


def backward(a1, a1t, h1, dy, a0t, gu, wd0, w_gate, w_up, w_down):
    pair = ((2, 2, 4, 112, WIDE), (2, 4, 64, D))
    two = ((2, 2, 2, 112, WIDE), (2, 2, 64, D))
    one = ((2, 2, 112, WIDE), (2, 64, D))
    return pl.pallas_call(
        backward_kernel,
        name="backward",
        out_shape=[shape((2, 112, FF)), shape((2, 112, FF)), shape((2, 7, 64, D)), shape((1, WIDE), F32), shape((1, D), F32)],
        in_specs=[ANY] * 10,
        out_specs=[ANY] * 3 + [pl.BlockSpec(memory_space=pltpu.VMEM)] * 2,
        scratch_shapes=[
            pltpu.VMEM((TILES, 2, 8, 112, WIDE), BF16), pltpu.VMEM((4, 14, 64, D), BF16), pltpu.VMEM((T, D), BF16), pltpu.VMEM((2, 448, T), BF16),
            pltpu.VMEM((T, D), BF16), pltpu.VMEM((T, D), F32), *[pltpu.VMEM((T, WIDE), BF16)] * 3,
            pltpu.VMEM((3, 2, 4, 2, 112, WIDE), BF16), pltpu.VMEM((3, 4, 2, 64, D), BF16),
            *[pltpu.VMEM(dims, BF16) for dims in (*pair, *two, *one, *one, *one)],
            sems(3), sems(TILES + 1), sems(2, 2), *GATHER_SEMS,
            sems(2, 2), sems(2, 2), sems(6, 2), sems(6, 2), sems(3, 2), sems(3, 2), sems(2, 2), sems(2, 2), sems(2), sems(2), sems(2), sems(STEPS),
            *[pltpu.SemaphoreType.REGULAR] * 6,
        ],
        compiler_params=pltpu.CompilerParams(collective_id=1, has_side_effects=True, vmem_limit_bytes=VMEM_LIMIT),
    )(a1, a1t, h1, dy, a0t, gu, wd0, w_gate, w_up, w_down)


def adamw(w, m, v, g):
    m = 0.9 * m + 0.1 * g
    v = 0.95 * v + 0.05 * g * g
    step = m * lax.rsqrt(v + 1e-8) + 0.1 * w
    return (w - 0.02 * step).astype(BF16), m, v


def solution(mesh):
    def step(x, dy, *arrays):
        weights, m, v = (arrays[i : i + 3] for i in (0, 3, 6))
        shards = (weights[0], weights[1], weights[2].reshape(2, 7, 64, D))
        gu, a0t, h1, a1, a1t, wd0 = forward(x[0], *shards)
        *gradients, squares, squares_down = backward(a1, a1t, h1, dy[0], a0t, gu, wd0, *shards)
        gradients[2] = gradients[2].reshape(2, 448, D)
        squares = lax.psum(jnp.sum(squares) + jnp.sum(squares_down), "s")
        count = lax.psum(1, "s") * sum(g.size for g in gradients)
        factor = jnp.minimum(1.0, 0.5 * lax.rsqrt(squares / count + 1e-30))
        new = [adamw(w.astype(F32), m, v, g.astype(F32) * factor) for w, m, v, g in zip(weights, m, v, gradients, strict=True)]
        return tuple(one[which] for which in range(3) for one in new)

    states, cut = P(("rep", "r", "s"), None, None), P(None, "s", None)
    return jax.shard_map(
        step,
        mesh=mesh,
        in_specs=(states, states) + (cut,) * 9,
        out_specs=(P("rep", "s", None),) * 9,
        check_vma=False,
    )
```

time: 920 us -> 499 us (0.54)
  Pallas kernels: 0 us -> 461 us
  waiting for transfers between devices: 445 us -> 0 us
  matrix products: 380 us -> 0 us
  local copies, waits for them, and re-layouts: 25.4 us -> 0.48 us
  between operations: 17 us -> 2.7 us
  other arithmetic: 30 us -> 20.5 us
    pallas_call x0 -> x2, Pallas kernels: none -> 461 us  [the longest x1 352 us: backward(): pl.pallas_call(backward_kernel, name='backward', out_shape=[shape((2, 112...]
    dot_general x15 -> x0, matrix products: 380 us -> none  [the longest x5 140 us: layer(): gate = jnp.dot(a, w['w_gate'], preferred_element_type=jnp.float32)]
    reduce_scatter x6 -> x0, waiting for transfers between devices: 203 us -> none  [summed(): lax.psum_scatter(term, 's', scatter_dimension=0, tiled=True)]
    psum x1 -> x0, waiting for transfers between devices: 121 us -> none  [summed(): lax.psum(lax.psum_scatter(term, 's', scatter_dimension=0, tiled=True), 'r')]
    all_gather x6 -> x0, waiting for transfers between devices: 120 us -> none  [fetched(): lax.all_gather(w[number], 's', axis=0, tiled=True)]
    unnamed x42 -> x12, local copies, waits for them, and re-layouts: 18.7 us -> 0.48 us
  transfers between devices with their start and end apart: 13 -> 0, of which waited for: 11 -> 0; matrix products, arithmetic and copies ran while one was open for 32% -> 0% of each run, Pallas kernels for 0% -> 0%
where the time goes in v1:
time: 499 us
  Pallas kernels  461 us (92%)
  other arithmetic  20.5 us (4%)
  blocking collectives  13.6 us (3%)
    pallas_call x1, Pallas kernels, backward(): pl.pallas_call(backward_kernel, name='backward', out_shape=[shape((2, 112...  352 us
    pallas_call x1, Pallas kernels, forward(): pl.pallas_call(forward_kernel, name='forward', out_shape=[shape((TILES, 2...  109 us
    convert_element_type x2, other arithmetic, adamw(): return ((w - 0.02 * step).astype(BF16), m, v)  15.9 us
    psum x1, blocking collectives, step(): squares = lax.psum(jnp.sum(squares) + jnp.sum(squares_down), 's')  13.6 us

profile of v1, /device:TPU:0, one launch (start us, length us, event | category | flops | bytes accessed | tf_op | source)
XLA Modules:
  0.0 498.6 jit_solution(17253562340091381822)
XLA Ops:
  0.6 109.5 %forward.1 = (f32[7,2,2048,512]{3,2,1,0:T(8,128)}, bf16[2,448,2048]{2,1,0:T(8,128)(2,1)}, bf16[2048,896]{1,0:T(8,128)(2,1)}, bf16[2048,896]{1,0:T(8,128)(2,1)}, ...) custom-call(bf16[2048,896]{1,0:T(8,128)(2,1)} %bitcast.12, bf16[2,112,3584]{2,1,0:T(8,128)(2,1)} %wg_h.3, ...), custom_call_target="tpu_custom_call" | custom-call | tf_op jit(solution)/shard_map/forward/pallas_call | solution.py:594
  110.1 351.8 %backward.1 = (bf16[2,112,3584]{2,1,0:T(8,128)(2,1)}, bf16[2,112,3584]{2,1,0:T(8,128)(2,1)}, bf16[2,7,64,896]{3,2,1,0:T(8,128)(2,1)}, f32[1,512]{1,0:T(1,128)}, f32[1,896]{1,0:T(1,128)}) custom-call(bf16[2048,896]{1,0:T(8,128)(2,1)} %get-tuple-element.20.a1_h, bf16[2,448,2048]{2,1,0:T(8,128)(2,1)} %get-tuple-element.21.a1t_h, ...), custom_call_target="tpu_custom_call" | custom-call | tf_op jit(solution)/shard_map/backward/pallas_call | solution.py:615
  461.9 0.0 copy-start.2
  461.9 1.4 reduce_sum.19
  463.3 1.3 reduce_sum.18
  465.9 13.6 %psum.7 = f32[]{:T(128)} all-reduce(f32[]{:T(128)S(6)} %add.47), channel_id=1, replica_groups=mesh['rep'=1,'r'=2,'s'=8] {'s'}, use_global_device_ids=true, to_apply=%region_2.0 | all-reduce | flops 1 | bytes 8 | tf_op jit(solution)/shard_map/psum | solution.py:648
  480.2 0.0 copy-start.3
  480.3 1.9 convert_multiply_fusion.3
  482.2 0.0 copy-done.2
  482.2 0.5 copy-done.3
  482.6 0.0 copy-start
  482.6 0.0 copy-start.1
  482.6 0.0 copy-start.4
  482.6 0.0 copy-start.5
  482.7 6.5 %fusion.8 = (bf16[2,448,896]{2,1,0:T(8,128)(2,1)}, f32[2,448,896]{2,1,0:T(8,128)}, f32[2,448,896]{2,1,0:T(8,128)}) fusion(bf16[2,448,896]{2,1,0:T(8,128)(2,1)S(1)} %copy-done.2, f32[2,7,64,896]{3,2,1,0:T(8,128)S(1)} %convert_multiply_fusion.3, f32[2,448,896]{2,1,0:T(8,128)S(1)} %copy-done.3, f32[2,448,896]{2,1,0:T(8,128)} %param.18), kind=kLoop, calls=%fused_computation.17 | loop fusion | flops 12042240 | bytes 19267584 | tf_op jit(solution)/shard_map/convert_element_type | solution.py:638
  489.2 0.0 copy-done
  489.2 0.0 copy-done.1
  489.2 0.0 copy-done.4
  489.2 0.0 copy-done.5
  489.2 9.4 %fusion.2 = (bf16[2,112,3584]{2,1,0:T(8,128)(2,1)}, f32[2,112,3584]{2,1,0:T(8,128)}, f32[2,112,3584]{2,1,0:T(8,128)}, bf16[2,112,3584]{2,1,0:T(8,128)(2,1)}, f32...) fusion(bf16[2,112,3584]{2,1,0:T(8,128)(2,1)S(1)} %copy-done, f32[]{:T(128)S(6)} %min_shard_map.3, ...), kind=kLoop, calls=%fused_computation.11 | loop fusion | flops 27295744 | bytes 35323908 | tf_op jit(solution)/shard_map/convert_element_type | solution.py:638
Async XLA Ops:
  461.9 20.3 %copy-start.2 = (bf16[2,448,896]{2,1,0:T(8,128)(2,1)S(1)}, bf16[2,448,896]{2,1,0:T(8,128)(2,1)}, u32[]{:S(2)}) copy-start(bf16[2,448,896]{2,1,0:T(8,128)(2,1)} %param.15) | copy-start | bytes 4816900
  480.2 2.4 copy-start.3
  482.6 6.5 %copy-start = (bf16[2,112,3584]{2,1,0:T(8,128)(2,1)S(1)}, bf16[2,112,3584]{2,1,0:T(8,128)(2,1)}, u32[]{:S(2)}) copy-start(bf16[2,112,3584]{2,1,0:T(8,128)(2,1)} %wg_h.3) | copy-start | bytes 4816900
  482.6 6.5 %copy-start.1 = (bf16[2,112,3584]{2,1,0:T(8,128)(2,1)S(1)}, bf16[2,112,3584]{2,1,0:T(8,128)(2,1)}, u32[]{:S(2)}) copy-start(bf16[2,112,3584]{2,1,0:T(8,128)(2,1)} %wu_h.3) | copy-start | bytes 4816900
  482.6 6.5 %copy-start.4 = (f32[2,112,3584]{2,1,0:T(8,128)S(1)}, f32[2,112,3584]{2,1,0:T(8,128)}, u32[]{:S(2)}) copy-start(f32[2,112,3584]{2,1,0:T(8,128)} %param.19) | copy-start | bytes 9633796
  482.6 6.5 %copy-start.5 = (bf16[2,112,3584]{2,1,0:T(8,128)(2,1)S(1)}, bf16[2,112,3584]{2,1,0:T(8,128)(2,1)}, u32[]{:S(2)}) copy-start(bf16[2,112,3584]{2,1,0:T(8,128)(2,1)} %get-tuple-element.26) | copy-start | bytes 4816900

commit v2 on v1

--- a/solution.py
+++ b/solution.py
@@ -10,6 +10,7 @@
 TILES, WIDE, ROWS = 7, 512, 512
 BLOCKS = T // ROWS
 STEPS = 2 * TILES
+SLOTS = 4
 F32, BF16 = jnp.float32, jnp.bfloat16
 VMEM_LIMIT = 67_043_328
 ANY = pl.BlockSpec(memory_space=pl.ANY)
@@ -27,6 +28,10 @@
 
 def block(i):
     return pl.ds(pl.multiple_of(i * ROWS, ROWS), ROWS)
+
+
+def tile_of(j):
+    return (j % 2) * 4 + j // 2
 
 
 class Place:
@@ -44,12 +49,16 @@
         self.to_a, self.to_b = {"s": self.sa}, {"s": self.sb}
         self.to_x, self.to_y, self.to_c, self.to_z = {"s": self.sx}, {"s": self.sy}, {"s": self.sc}, {"r": 1 - r}
 
+    def plane(self, n):
+        return {"s": (self.s + n) % 8}
+
 
 def barrier(at):
     sem = pltpu.get_barrier_semaphore()
-    for to in (at.to_x, at.to_y, at.to_c, at.to_z):
+    partners = [at.plane(n) for n in range(1, 8)] + [at.to_z]
+    for to in partners:
         pl.semaphore_signal(sem, inc=1, device_id=to, device_id_type=MESH)
-    pl.semaphore_wait(sem, 4)
+    pl.semaphore_wait(sem, len(partners))
 
 
 class Gather:
@@ -96,11 +105,11 @@
 
 
 def load_own(at, layer, wg_h, wu_h, wd_h, WGU, WD, own):
-    for i in range(TILES):
+    for j in range(TILES):
         for which, w in enumerate((wg_h, wu_h)):
             for k in range(4):
                 pltpu.make_async_copy(
-                    w.at[layer, :, pl.ds(k * 896 + i * 128, 128)], WGU.at[i, which, at.s, :, pl.ds(k * 128, 128)], own.at[i]
+                    w.at[layer, :, pl.ds(k * 896 + tile_of(j) * 128, 128)], WGU.at[j, which, at.s, :, pl.ds(k * 128, 128)], own.at[j]
                 ).start()
     pltpu.make_async_copy(wd_h.at[layer], WD.at[at.q, pl.ds(at.c * 7, 7)], own.at[TILES]).start()
 
@@ -123,14 +132,14 @@
     return WGU[i, which].reshape(D, WIDE)
 
 
-def down_tile(WD, i):
-    return WD[:, pl.ds(2 * i, 2)].reshape(WIDE, D)
+def down_tile(WD, j):
+    return WD[:, pl.ds(2 * tile_of(j), 2)].reshape(WIDE, D)
 
 
 def forward_kernel(
     x_h, wg_h, wu_h, wd_h,
     gu_o, a0t_o, h1_o, a1_o, a1t_o, wd_o,
-    WGU, WD, X, A, AT, MID, ST,
+    WGU, WD, X, A, AT, MID, ST, ACC,
     load, own, stage, out, sgu, rgu, sd, rd,
 ):
     at = Place()
@@ -160,48 +169,62 @@
     a0t_out = pltpu.make_async_copy(AT, a0t_o, out.at[0])
     a0t_out.start()
     gu.first(0)
-
-    def staged(i, m, slot):
-        return pltpu.make_async_copy(ST.at[slot], gu_o.at[i, :, block(m), :], stage.at[slot])
-
-    def tile(i, _):
-        pl.when(i < TILES - 1)(lambda: gu.first(i + 1))
-        gu.second(i)
-        gu.whole(i)
+    gu.first(1)
+    gu.second(0)
+
+    def staged(j, m, slot):
+        return pltpu.make_async_copy(ST.at[slot], gu_o.at[j, :, block(m), :], stage.at[slot])
+
+    def tile(j, _):
+        gu.whole(j)
+        pl.when(j < TILES - 2)(lambda: gu.first(j + 2))
+        pl.when(j >= TILES - 2)(lambda: down.first(j - TILES + 2))
 
         def rows(m, _):
+            @pl.when(m == 2)
+            def _():
+                pl.when(j < TILES - 1)(lambda: gu.second(j + 1))
+                pl.when(j == TILES - 1)(lambda: down.second(0))
+
             slot = m % 2
-            pl.when(i * BLOCKS + m >= 2)(lambda: staged(i, m, slot).wait())
+            pl.when(j * BLOCKS + m >= 2)(lambda: staged(j, m, slot).wait())
             a = A[block(m), :]
-            gate = dot(a, gate_up(WGU, i, 0))
-            up = dot(a, gate_up(WGU, i, 1))
+            gate = dot(a, gate_up(WGU, j, 0))
+            up = dot(a, gate_up(WGU, j, 1))
             ST[slot, 0] = gate
             ST[slot, 1] = up
-            staged(i, m, slot).start()
-            MID[i, block(m), :] = (gate * jax.nn.sigmoid(gate) * up).astype(BF16)
+            staged(j, m, slot).start()
+            MID[j, block(m), :] = (gate * jax.nn.sigmoid(gate) * up).astype(BF16)
             return 0
 
         return lax.fori_loop(0, BLOCKS, rows, 0)
 
     lax.fori_loop(0, TILES, tile, 0)
-    down.first(0)
-
-    def piece(n, _):
-        pl.when(n < TILES - 1)(lambda: down.first(n + 1))
-        down.second(n)
-        down.whole(n)
-        return 0
-
-    lax.fori_loop(0, TILES, piece, 0)
+    down.whole(0)
+    down.first(2)
+    down.second(1)
+
+    def below(j, _):
+        down.whole(j + 1)
+        pl.when(j < TILES - 3)(lambda: down.first(j + 3))
+
+        def rows(m, _):
+            pl.when((m == 2) & (j < TILES - 2))(lambda: down.second(j + 2))
+            part = dot(MID[j, block(m), :], down_tile(WD, j))
+            ACC[block(m), :] += part
+            return 0
+
+        return lax.fori_loop(0, BLOCKS, rows, 0)
+
+    ACC[...] = jnp.zeros_like(ACC)
+    lax.fori_loop(0, TILES - 1, below, 0)
     wd_out = pltpu.make_async_copy(WD, wd_o, out.at[1])
     wd_out.start()
     a0t_out.wait()
 
     def finish(m, _):
-        total = dot(MID[0, block(m), :], down_tile(WD, 0))
-        for i in range(1, TILES):
-            total += dot(MID[i, block(m), :], down_tile(WD, i))
-        h = (X[block(m), :].astype(F32) + total.astype(BF16).astype(F32)).astype(BF16)
+        total = ACC[block(m), :] + dot(MID[TILES - 1, block(m), :], down_tile(WD, TILES - 1))
+        h = added(X[block(m), :], total.astype(BF16))
         X[block(m), :] = h
         a = normed(h)
         A[block(m), :] = a
@@ -232,9 +255,9 @@
 
 def backward_kernel(
     a1_h, a1t_h, h1_h, dy_h, a0t_h, gu_h, wd0_h, wg_h, wu_h, wd_h,
-    gg_o, gu_o, gd_o, sqw_o, sqd_o,
-    WGU, WD, A, AT, DY, ACC, MID, DG, DU, TW, TD, RW, RD, FW, FD, BW, BD, ZW, ZD, OW, OD,
-    load, own, gus, sgu, rgu, sd, rd, pair_s, pair_r, first_s, first_r, second_s, second_r, z_s, z_r, ow_s, od_s, od_remote_s, od_r,
+    gg_o, gu_o, gd_o, sq_o,
+    WGU, WD, A, AT, DY, ACC, MID, DG, DU, TW, TD, RW, RD, FW, FD, BW, BD, ZW, ZD, OW, OD, SQW, SQD, SQ,
+    load, own, gus, sgu, rgu, sd, rd, pair_s, pair_r, first_s, first_r, second_s, second_r, z_s, z_r, ow_s, od_s, od_remote_s, od_r, sq_s, sq_r,
     pair_free, first_x, first_y, second_x, second_y, z_free,
 ):
     at = Place()
@@ -249,26 +272,24 @@
     barrier(at)
     gather, down = gathers(at, WGU, WD, sgu, rgu, sd, rd)
     wait_own_down(at, wd_h, 1, WD, own)
-    lax.fori_loop(0, TILES, lambda n, _: (down.own(n), 0)[1], 0)
-
-    def start_tile(n, _):
-        wait_own_tile(at, n, WGU, own)
-        gather.own(n)
+    down.own(0)
+
+    def start_tile(j, _):
+        pl.when(j < TILES - 1)(lambda: down.own(j + 1))
+        wait_own_tile(at, j, WGU, own)
+        gather.own(j)
         return 0
 
     lax.fori_loop(0, TILES, start_tile, 0)
-    sqw_o[...] = jnp.zeros_like(sqw_o)
-    sqd_o[...] = jnp.zeros_like(sqd_o)
+    SQW[...] = jnp.zeros_like(SQW)
+    SQD[...] = jnp.zeros_like(SQD)
+    ACC[...] = jnp.zeros_like(ACC)
     down.first(0)
-
-    def piece(n, _):
-        pl.when(n < TILES - 1)(lambda: down.first(n + 1))
-        down.second(n)
-        return 0
-
-    lax.fori_loop(0, TILES, piece, 0)
+    down.first(1)
+    down.second(0)
     gather.first(0)
-    lax.fori_loop(0, TILES, lambda n, _: (down.whole(n), 0)[1], 0)
+    down.second(1)
+    down.whole(0)
     gather.second(0)
     for one in loads:
         one.wait()
@@ -276,127 +297,102 @@
     def remote(src, dst, send, recv, to):
         return pltpu.make_async_remote_copy(src_ref=src, dst_ref=dst, send_sem=send, recv_sem=recv, device_id=to, device_id_type=MESH)
 
-    def credit(sem, to):
-        pl.semaphore_signal(sem, inc=1, device_id=to, device_id_type=MESH)
-
-    def pair_copies(t):
-        k, j = t % 3, t % 2
-        return [
-            remote(TW.at[k, :, :, 1 - c], RW.at[j], pair_s.at[0, j], pair_r.at[0, j], at.to_c),
-            remote(TD.at[k, :, 1 - c], RD.at[j], pair_s.at[1, j], pair_r.at[1, j], at.to_c),
-        ]
-
-    def pair_send(t):
-        pl.when(t >= 2)(lambda: pl.semaphore_wait(pair_free, 1))
-        for one in pair_copies(t):
-            one.start()
-
-    def pair_add(t):
-        k, j = t % 3, t % 2
-        for one in pair_copies(t):
-            one.wait()
-
-        def chip(p, _):
-            for which in range(2):
-                TW[k, which, p, c] = added(TW[k, which, p, c], RW[j, which, p])
-            TD[k, p, c] = added(TD[k, p, c], RD[j, p])
-            return 0
-
-        lax.fori_loop(0, 4, chip, 0)
-        pl.when(t < STEPS - 2)(lambda: credit(pair_free, at.to_c))
-
-    def ways(t):
-        turn = t % 2
-        x, y = (at.sx, qx), (at.sy, qy)
-        mixed = tuple(a + turn * (b - a) for a, b in zip(x, y))
-        other = tuple(b + turn * (a - b) for a, b in zip(x, y))
-        return (x, y), (y, x), (mixed, other)
-
-    def buffers(t, which):
-        k, j = t % 3, t % 2
-        if which < 2:
-            return (lambda p: TW.at[k, which, p, c]), (lambda n: FW.at[j, which, n]), BW.at[j, which]
-        return (lambda p: TD.at[k, p, c]), (lambda n: FD.at[j, n]), BD.at[j]
-
-    def first_copies(t):
-        j, copies = t % 2, []
-        for which, (one, _) in enumerate(ways(t)):
-            mine, into, _ = buffers(t, which)
-            for n, p in enumerate((one[1], qd)):
-                copies.append(remote(mine(p), into(n), first_s.at[2 * which + n, j], first_r.at[2 * which + n, j], {"s": one[0]}))
-        return copies
-
-    def first_send(t):
+    def pair_copy(t, one):
+        k, j = t % SLOTS, t % 2
+        src, dst = (TW.at[k, one, :, 1 - c], RW.at[j, one]) if one < 2 else (TD.at[k, :, 1 - c], RD.at[j])
+        return remote(src, dst, pair_s.at[one, j], pair_r.at[one, j], at.to_c)
+
+    def buffers(t, part):
+        k, j = t % SLOTS, t % 2
+        if part < 2:
+            return (lambda p: TW.at[k, part, p, c]), (lambda n: FW.at[j, part, n]), BW.at[j, part]
+        rows = pl.ds(32 * (part - 2), 32)
+        return (lambda p: TD.at[k, p, c, rows]), (lambda n: FD.at[j, n, rows]), BD.at[j, rows]
+
+    x, y = (at.to_x, qx), (at.to_y, qy)
+
+    def ways(part):
+        return (x, y) if part % 2 == 0 else (y, x)
+
+    def first_copies(t, part):
+        mine, into, _ = buffers(t, part)
+        to, near = ways(part)[0]
+        return [remote(mine(p), into(n), first_s.at[2 * part + n, t % 2], first_r.at[2 * part + n, t % 2], to) for n, p in enumerate((near, qd))]
+
+    def second_copy(t, part):
+        mine, _, into = buffers(t, part)
+        to, near = ways(part)[1]
+        return remote(mine(near), into, second_s.at[part, t % 2], second_r.at[part, t % 2], to)
+
+    def z_copy(t, one):
+        k, j = t % SLOTS, t % 2
+        src, dst = (TW.at[k, one, q, c], ZW.at[j, one]) if one < 2 else (TD.at[k, q, c], ZD.at[j])
+        return remote(src, dst, z_s.at[one, j], z_r.at[one, j], at.to_z)
+
+    def spend(t, *sems):
         @pl.when(t >= 2)
         def _():
-            pl.semaphore_wait(first_x, 1)
-            pl.semaphore_wait(first_y, 1)
-
-        for one in first_copies(t):
-            one.start()
-
-    def first_add(t):
-        for one in first_copies(t):
-            one.wait()
-        for which, (_, two) in enumerate(ways(t)):
-            mine, into, _ = buffers(t, which)
-            for n, p in enumerate((q, two[1])):
-                mine(p)[...] = added(mine(p)[...], into(n)[...])
-
+            for sem in sems:
+                pl.semaphore_wait(sem, 1)
+
+    def free(t, *pairs):
         @pl.when(t < STEPS - 2)
         def _():
-            credit(first_x, at.to_x)
-            credit(first_y, at.to_y)
-
-    def second_copies(t):
-        j, copies = t % 2, []
-        for which, (_, two) in enumerate(ways(t)):
-            mine, _, into = buffers(t, which)
-            copies.append(remote(mine(two[1]), into, second_s.at[which, j], second_r.at[which, j], {"s": two[0]}))
-        return copies
-
-    def second_send(t):
-        @pl.when(t >= 2)
-        def _():
-            pl.semaphore_wait(second_x, 1)
-            pl.semaphore_wait(second_y, 1)
-
-        for one in second_copies(t):
-            one.start()
-
-    def second_add(t):
-        for one in second_copies(t):
-            one.wait()
-        for which in range(3):
-            mine, _, into = buffers(t, which)
-            mine(q)[...] = added(mine(q)[...], into[...])
-
-        @pl.when(t < STEPS - 2)
-        def _():
-            credit(second_x, at.to_x)
-            credit(second_y, at.to_y)
-
-    def z_copies(t):
-        k, j = t % 3, t % 2
-        return [
-            remote(TW.at[k, :, q, c], ZW.at[j], z_s.at[0, j], z_r.at[0, j], at.to_z),
-            remote(TD.at[k, q, c], ZD.at[j], z_s.at[1, j], z_r.at[1, j], at.to_z),
-        ]
-
-    def z_send(t):
-        pl.when(t >= 2)(lambda: pl.semaphore_wait(z_free, 1))
-        for one in z_copies(t):
-            one.start()
+            for sem, to in pairs:
+                pl.semaphore_signal(sem, inc=1, device_id=to, device_id_type=MESH)
+
+    PARTS = ((0,), (1,), (2, 3))
+
+    def stage_one(t):
+        k, j = t % SLOTS, t % 2
+        spend(t, first_x, first_y)
+        for one in range(3):
+            pair_copy(t, one).wait()
+
+            def chip(p, _):
+                if one < 2:
+                    TW[k, one, p, c] = added(TW[k, one, p, c], RW[j, one, p])
+                else:
+                    TD[k, p, c] = added(TD[k, p, c], RD[j, p])
+                return 0
+
+            lax.fori_loop(0, 4, chip, 0)
+            for part in PARTS[one]:
+                for copy in first_copies(t, part):
+                    copy.start()
+        free(t, (pair_free, at.to_c))
+
+    def stage_two(t):
+        spend(t, second_x, second_y)
+        for part in range(4):
+            for copy in first_copies(t, part):
+                copy.wait()
+            mine, into, _ = buffers(t, part)
+            other = ways(part)[1][1]
+            mine(other)[...] = added(mine(other)[...], into(1)[...])
+            second_copy(t, part).start()
+            mine(q)[...] = added(mine(q)[...], into(0)[...])
+        free(t, (first_x, at.to_x), (first_y, at.to_y))
+
+    def stage_three(t):
+        spend(t, z_free)
+        for one in range(3):
+            for part in PARTS[one]:
+                second_copy(t, part).wait()
+                mine, _, into = buffers(t, part)
+                mine(q)[...] = added(mine(q)[...], into[...])
+            z_copy(t, one).start()
+        free(t, (second_x, at.to_x), (second_y, at.to_y))
 
     def half(t, core):
-        number = (t % TILES) * 2 + core
+        number = tile_of(t % TILES) * 2 + core
         return number // 7, number % 7
 
     def layer_of(t):
         return 1 - t // TILES
 
     def wide_out(t):
-        j, i = t % 2, t % TILES
+        j, i = t % 2, tile_of(t % TILES)
         for which, o in enumerate((gg_o, gu_o)):
             for k in range(4):
                 lanes = pl.ds(pl.multiple_of(k * 896 + i * 128, 128), 128)
@@ -424,21 +420,20 @@
         pl.when(owner == c)(lambda: down_local(t).wait())
         pl.when(owner != c)(lambda: down_remote(t, c).wait_send())
 
-    def z_add(t):
-        k, j = t % 3, t % 2
+    def stage_four(t):
+        k, j = t % SLOTS, t % 2
         pl.when(t >= 2)(lambda: out_wait(t - 2))
-        for one in z_copies(t):
-            one.wait()
-        for which in range(2):
-            g = added(TW[k, which, q, c], ZW[j, which])
-            OW[j, which] = g
+        for one in range(3):
+            z_copy(t, one).wait()
+            g = added(TW[k, one, q, c], ZW[j, one]) if one < 2 else added(TD[k, q, c], ZD[j])
             wide = g.astype(F32)
-            sqw_o[...] += jnp.sum(wide * wide, 0, keepdims=True)
-        g = added(TD[k, q, c], ZD[j])
-        OD[j] = g
-        wide = g.astype(F32)
-        sqd_o[...] += jnp.sum(wide * wide, 0, keepdims=True)
-        pl.when(t < STEPS - 2)(lambda: credit(z_free, at.to_z))
+            if one < 2:
+                OW[j, one] = g
+                SQW[...] += jnp.sum((wide * wide).reshape(14, 8, WIDE), 0)
+            else:
+                OD[j] = g
+                SQD[...] += jnp.sum((wide * wide).reshape(8, 8, D), 0)
+        free(t, (z_free, at.to_z))
         out_start(t)
 
     def between(gate, up, by_mid):
@@ -452,14 +447,15 @@
             ref[block(m), :] = value
 
     def layer_one(i):
+        pl.when(i < TILES - 1)(lambda: down.whole(i + 1))
         gather.whole(i)
-        pl.when(i < TILES - 1)(lambda: gather.first(i + 1))
-
-        @pl.when(i == 0)
-        def _():
-            ACC[...] = jnp.zeros_like(ACC)
 
         def rows(m, _):
+            @pl.when((m == 2) & (i < TILES - 1))
+            def _():
+                pl.when(i < TILES - 2)(lambda: down.first(i + 2))
+                gather.first(i + 1)
+
             a = A[block(m), :]
             gate = dot(a, gate_up(WGU, i, 0))
             up = dot(a, gate_up(WGU, i, 1))
@@ -519,22 +515,32 @@
         lax.fori_loop(0, BLOCKS, rows, 0)
 
     def gradients(t):
-        k = t % 3
-
-        def rows(half, _):
-            for which, by in enumerate((DG, DU)):
+        k = t % SLOTS
+        spend(t, pair_free)
+        for which, by in enumerate((DG, DU)):
+
+            def rows(half, _):
                 TW[k, which, pl.ds(2 * half, 2)] = dot(AT[half], by[...]).astype(BF16).reshape(2, 2, 112, WIDE)
-            return 0
-
-        lax.fori_loop(0, 2, rows, 0)
+                return 0
+
+            lax.fori_loop(0, 2, rows, 0)
+            pair_copy(t, which).start()
         TD[k] = dot(MID[...], DY[...], (0, 0)).astype(BF16).reshape(4, 2, 64, D)
+        pair_copy(t, 2).start()
 
     def step(t, _):
         pl.when(t < TILES)(lambda: layer_one(t))
         pl.when(t == TILES)(turn)
         pl.when((t >= TILES) & (t < STEPS))(lambda: layer_zero(t - TILES))
-
-        pl.when(t < TILES - 1)(lambda: gather.second(t + 1))
+        pl.when((t >= 1) & (t <= STEPS))(lambda: stage_one(t - 1))
+        pl.when((t >= 2) & (t <= STEPS + 1))(lambda: stage_two(t - 2))
+        pl.when((t >= 3) & (t <= STEPS + 2))(lambda: stage_three(t - 3))
+        pl.when(t >= 4)(lambda: stage_four(t - 4))
+
+        @pl.when(t < TILES - 1)
+        def _():
+            pl.when(t < TILES - 2)(lambda: down.second(t + 2))
+            gather.second(t + 1)
 
         @pl.when(t == TILES - 1)
         def _():
@@ -542,30 +548,19 @@
             lax.fori_loop(0, TILES, lambda n, _: (down.sent(n), 0)[1], 0)
             wd0_in.start()
 
-        @pl.when((t >= 1) & (t <= STEPS))
-        def _():
-            pair_add(t - 1)
-            first_send(t - 1)
-
-        @pl.when(t >= 2)
-        def _():
-            second_add(t - 2)
-            z_send(t - 2)
-
-        @pl.when(t < STEPS)
-        def _():
-            gradients(t)
-            pair_send(t)
-
-        @pl.when((t >= 1) & (t <= STEPS))
-        def _():
-            first_add(t - 1)
-            second_send(t - 1)
-
-        pl.when(t >= 2)(lambda: z_add(t - 2))
+        pl.when(t < STEPS)(lambda: gradients(t))
         return 0
 
-    lax.fori_loop(0, STEPS + 2, step, 0)
+    lax.fori_loop(0, STEPS + 4, step, 0)
+
+    mine = jnp.sum(SQW[...], keepdims=True) + jnp.sum(SQD[...], keepdims=True)
+    SQ[at.s] = jnp.broadcast_to(mine, (8, 128))
+
+    def square(n, from_):
+        return remote(SQ.at[from_], SQ.at[from_], sq_s.at[n - 1], sq_r.at[n - 1], at.plane(n))
+
+    for n in range(1, 8):
+        square(n, at.s).start()
     out_wait(STEPS - 2)
     out_wait(STEPS - 1)
 
@@ -577,6 +572,13 @@
         return 0
 
     lax.fori_loop(0, STEPS, arrived, 0)
+    for n in range(1, 8):
+        square(n, (at.s + 8 - n) % 8).wait_recv()
+        square(n, at.s).wait_send()
+    total = SQ[0]
+    for n in range(1, 8):
+        total += SQ[n]
+    sq_o[...] = total
 
 
 def shape(dims, dtype=BF16):
@@ -601,7 +603,7 @@
         out_specs=[ANY] * 6,
         scratch_shapes=[
             pltpu.VMEM((TILES, 2, 8, 112, WIDE), BF16), pltpu.VMEM((4, 14, 64, D), BF16), pltpu.VMEM((T, D), BF16), pltpu.VMEM((T, D), BF16),
-            pltpu.VMEM((2, 448, T), BF16), pltpu.VMEM((TILES, T, WIDE), BF16), pltpu.VMEM((2, 2, ROWS, WIDE), F32),
+            pltpu.VMEM((2, 448, T), BF16), pltpu.VMEM((TILES, T, WIDE), BF16), pltpu.VMEM((2, 2, ROWS, WIDE), F32), pltpu.VMEM((T, D), F32),
             pltpu.SemaphoreType.DMA, sems(TILES + 1), sems(2), sems(5), *GATHER_SEMS,
         ],
         compiler_params=pltpu.CompilerParams(collective_id=0, has_side_effects=True, vmem_limit_bytes=VMEM_LIMIT),
@@ -615,16 +617,18 @@
     return pl.pallas_call(
         backward_kernel,
         name="backward",
-        out_shape=[shape((2, 112, FF)), shape((2, 112, FF)), shape((2, 7, 64, D)), shape((1, WIDE), F32), shape((1, D), F32)],
+        out_shape=[shape((2, 112, FF)), shape((2, 112, FF)), shape((2, 7, 64, D)), shape((8, 128), F32)],
         in_specs=[ANY] * 10,
-        out_specs=[ANY] * 3 + [pl.BlockSpec(memory_space=pltpu.VMEM)] * 2,
+        out_specs=[ANY] * 3 + [pl.BlockSpec(memory_space=pltpu.VMEM)],
         scratch_shapes=[
             pltpu.VMEM((TILES, 2, 8, 112, WIDE), BF16), pltpu.VMEM((4, 14, 64, D), BF16), pltpu.VMEM((T, D), BF16), pltpu.VMEM((2, 448, T), BF16),
             pltpu.VMEM((T, D), BF16), pltpu.VMEM((T, D), F32), *[pltpu.VMEM((T, WIDE), BF16)] * 3,
-            pltpu.VMEM((3, 2, 4, 2, 112, WIDE), BF16), pltpu.VMEM((3, 4, 2, 64, D), BF16),
+            pltpu.VMEM((SLOTS, 2, 4, 2, 112, WIDE), BF16), pltpu.VMEM((SLOTS, 4, 2, 64, D), BF16),
             *[pltpu.VMEM(dims, BF16) for dims in (*pair, *two, *one, *one, *one)],
+            pltpu.VMEM((8, WIDE), F32), pltpu.VMEM((8, D), F32), pltpu.VMEM((8, 8, 128), F32),
             sems(3), sems(TILES + 1), sems(2, 2), *GATHER_SEMS,
-            sems(2, 2), sems(2, 2), sems(6, 2), sems(6, 2), sems(3, 2), sems(3, 2), sems(2, 2), sems(2, 2), sems(2), sems(2), sems(2), sems(STEPS),
+            sems(3, 2), sems(3, 2), sems(8, 2), sems(8, 2), sems(4, 2), sems(4, 2), sems(3, 2), sems(3, 2), sems(2), sems(2), sems(2), sems(STEPS),
+            sems(7), sems(7),
             *[pltpu.SemaphoreType.REGULAR] * 6,
         ],
         compiler_params=pltpu.CompilerParams(collective_id=1, has_side_effects=True, vmem_limit_bytes=VMEM_LIMIT),
@@ -643,11 +647,10 @@
         weights, m, v = (arrays[i : i + 3] for i in (0, 3, 6))
         shards = (weights[0], weights[1], weights[2].reshape(2, 7, 64, D))
         gu, a0t, h1, a1, a1t, wd0 = forward(x[0], *shards)
-        *gradients, squares, squares_down = backward(a1, a1t, h1, dy[0], a0t, gu, wd0, *shards)
+        *gradients, squares = backward(a1, a1t, h1, dy[0], a0t, gu, wd0, *shards)
         gradients[2] = gradients[2].reshape(2, 448, D)
-        squares = lax.psum(jnp.sum(squares) + jnp.sum(squares_down), "s")
-        count = lax.psum(1, "s") * sum(g.size for g in gradients)
-        factor = jnp.minimum(1.0, 0.5 * lax.rsqrt(squares / count + 1e-30))
+        count = mesh.shape["s"] * sum(g.size for g in gradients)
+        factor = jnp.minimum(1.0, 0.5 * lax.rsqrt(squares[0, 0] / count + 1e-30))
         new = [adamw(w.astype(F32), m, v, g.astype(F32) * factor) for w, m, v, g in zip(weights, m, v, gradients, strict=True)]
         return tuple(one[which] for which in range(3) for one in new)
 

time: 499 us -> 418 us (0.84)
  Pallas kernels: 461 us -> 397 us
  blocking collectives: 13.6 us -> 0 us
    pallas_call x1, Pallas kernels: 352 us -> 308 us  [backward(): pl.pallas_call(backward_kernel, name='backward', out_shape=[shape((2, 112...]
    pallas_call x1, Pallas kernels: 109 us -> 89.1 us  [forward(): pl.pallas_call(forward_kernel, name='forward', out_shape=[shape((TILES, 2...]
    psum x1 -> x0, blocking collectives: 13.6 us -> none  [step(): squares = lax.psum(jnp.sum(squares) + jnp.sum(squares_down), 's')]
where the time goes in v2:
time: 418 us; the launch traced here: 417 us
  Pallas kernels  397 us (95%)
  other arithmetic  17.5 us (4%)
    pallas_call x1, Pallas kernels, backward(): pl.pallas_call(backward_kernel, name='backward', out_shape=[shape((2, 112...  308 us
    pallas_call x1, Pallas kernels, forward(): pl.pallas_call(forward_kernel, name='forward', out_shape=[shape((TILES, 2...  89.1 us
    convert_element_type x2, other arithmetic, adamw(): return ((w - 0.02 * step).astype(BF16), m, v)  15.8 us

profile of v2, /device:TPU:0, one launch (start us, length us, event | category | flops | bytes accessed | tf_op | source)
XLA Modules:
  0.0 417.4 jit_solution(9787268102247830819)
XLA Ops:
  0.6 89.1 %forward.1 = (f32[7,2,2048,512]{3,2,1,0:T(8,128)}, bf16[2,448,2048]{2,1,0:T(8,128)(2,1)}, bf16[2048,896]{1,0:T(8,128)(2,1)}, bf16[2048,896]{1,0:T(8,128)(2,1)}, ...) custom-call(bf16[2048,896]{1,0:T(8,128)(2,1)} %bitcast.13, bf16[2,112,3584]{2,1,0:T(8,128)(2,1)} %wg_h.3, ...), custom_call_target="tpu_custom_call" | custom-call | tf_op jit(solution)/shard_map/forward/pallas_call | solution.py:596
  89.8 307.9 %backward.1 = (bf16[2,112,3584]{2,1,0:T(8,128)(2,1)}, bf16[2,112,3584]{2,1,0:T(8,128)(2,1)}, bf16[2,7,64,896]{3,2,1,0:T(8,128)(2,1)}, f32[8,128]{1,0:T(8,128)}) custom-call(bf16[2048,896]{1,0:T(8,128)(2,1)} %get-tuple-element.19.a1_h, bf16[2,448,2048]{2,1,0:T(8,128)(2,1)} %get-tuple-element.20.a1t_h, bf16[2048,896]{1,0:T(8,128)(2,1)} %get-tuple-element.21.h1_h, ...), custom_call_target="tpu_custom_call" | custom-call | tf_op jit(solution)/shard_map/backward/pallas_call | solution.py:617
  397.7 0.0 copy-start.2
  397.7 0.0 copy-start.3
  397.7 1.3 slice.3
  399.8 1.8 convert_multiply_fusion.3
  401.6 0.0 copy-done.2
  401.6 0.0 copy-done.3
  401.6 0.0 copy-start
  401.6 0.0 copy-start.1
  401.6 0.0 copy-start.4
  401.6 0.0 copy-start.5
  401.6 6.6 %fusion.8 = (bf16[2,448,896]{2,1,0:T(8,128)(2,1)}, f32[2,448,896]{2,1,0:T(8,128)}, f32[2,448,896]{2,1,0:T(8,128)}) fusion(bf16[2,448,896]{2,1,0:T(8,128)(2,1)S(1)} %copy-done.2, f32[2,7,64,896]{3,2,1,0:T(8,128)S(1)} %convert_multiply_fusion.3, f32[2,448,896]{2,1,0:T(8,128)S(1)} %copy-done.3, f32[2,448,896]{2,1,0:T(8,128)} %param.18), kind=kLoop, calls=%fused_computation.17 | loop fusion | flops 12042240 | bytes 19267584 | tf_op jit(solution)/shard_map/convert_element_type | solution.py:642
  408.2 0.0 copy-done
  408.2 0.0 copy-done.1
  408.2 0.0 copy-done.4
  408.2 0.0 copy-done.5
  408.2 9.2 %fusion.2 = (bf16[2,112,3584]{2,1,0:T(8,128)(2,1)}, f32[2,112,3584]{2,1,0:T(8,128)}, f32[2,112,3584]{2,1,0:T(8,128)}, bf16[2,112,3584]{2,1,0:T(8,128)(2,1)}, f32...) fusion(bf16[2,112,3584]{2,1,0:T(8,128)(2,1)S(1)} %copy-done, f32[]{:T(128)} %bitcast.3, ...), kind=kLoop, calls=%fused_computation.11 | loop fusion | flops 27295744 | bytes 35323908 | tf_op jit(solution)/shard_map/convert_element_type | solution.py:642
Async XLA Ops:
  397.7 3.9 copy-start.2
  397.7 3.9 copy-start.3
  401.6 6.6 %copy-start = (bf16[2,112,3584]{2,1,0:T(8,128)(2,1)S(1)}, bf16[2,112,3584]{2,1,0:T(8,128)(2,1)}, u32[]{:S(2)}) copy-start(bf16[2,112,3584]{2,1,0:T(8,128)(2,1)} %wg_h.3) | copy-start | bytes 4816900
  401.6 6.6 %copy-start.1 = (bf16[2,112,3584]{2,1,0:T(8,128)(2,1)S(1)}, bf16[2,112,3584]{2,1,0:T(8,128)(2,1)}, u32[]{:S(2)}) copy-start(bf16[2,112,3584]{2,1,0:T(8,128)(2,1)} %wu_h.3) | copy-start | bytes 4816900
  401.6 6.6 %copy-start.4 = (f32[2,112,3584]{2,1,0:T(8,128)S(1)}, f32[2,112,3584]{2,1,0:T(8,128)}, u32[]{:S(2)}) copy-start(f32[2,112,3584]{2,1,0:T(8,128)} %param.19) | copy-start | bytes 9633796
  401.6 6.6 %copy-start.5 = (f32[2,112,3584]{2,1,0:T(8,128)S(1)}, f32[2,112,3584]{2,1,0:T(8,128)}, u32[]{:S(2)}) copy-start(f32[2,112,3584]{2,1,0:T(8,128)} %param.16) | copy-start | bytes 9633796

commit v3 on v2

--- a/solution.py
+++ b/solution.py
@@ -10,6 +10,7 @@
 TILES, WIDE, ROWS = 7, 512, 512
 BLOCKS = T // ROWS
 STEPS = 2 * TILES
+AHEAD = 2
 SLOTS = 4
 F32, BF16 = jnp.float32, jnp.bfloat16
 VMEM_LIMIT = 67_043_328
@@ -18,6 +19,14 @@
 
 def dot(a, b, contract=(1, 0)):
     return lax.dot_general(a, b, (((contract[0],), (contract[1],)), ((), ())), preferred_element_type=F32)
+
+
+def loop(n, body):
+    def run(i, carry):
+        body(i)
+        return carry
+
+    lax.fori_loop(0, n, run, 0)
 
 
 def normed(h):
@@ -104,22 +113,19 @@
             self.copy(way, n, shard, to).wait_send()
 
 
-def load_own(at, layer, wg_h, wu_h, wd_h, WGU, WD, own):
-    for j in range(TILES):
-        for which, w in enumerate((wg_h, wu_h)):
-            for k in range(4):
-                pltpu.make_async_copy(
-                    w.at[layer, :, pl.ds(k * 896 + tile_of(j) * 128, 128)], WGU.at[j, which, at.s, :, pl.ds(k * 128, 128)], own.at[j]
-                ).start()
-    pltpu.make_async_copy(wd_h.at[layer], WD.at[at.q, pl.ds(at.c * 7, 7)], own.at[TILES]).start()
+def load_tile(at, layer, j, wg_h, wu_h, into, sem):
+    for which, w in enumerate((wg_h, wu_h)):
+        for k in range(4):
+            pltpu.make_async_copy(w.at[layer, :, pl.ds(k * 896 + tile_of(j) * 128, 128)], into.at[which, at.s, :, pl.ds(k * 128, 128)], sem).start()
+
+
+def own_down(at, layer, wd_h, WD, own):
+    skip = layer * AHEAD
+    return pltpu.make_async_copy(wd_h.at[layer, pl.ds(skip, 7 - skip)], WD.at[at.q, pl.ds(at.c * 7 + skip, 7 - skip)], own.at[TILES])
 
 
 def wait_own_tile(at, i, WGU, own):
     pltpu.make_async_copy(WGU.at[i, :, at.s], WGU.at[i, :, at.s], own.at[i]).wait()
-
-
-def wait_own_down(at, wd_h, layer, WD, own):
-    pltpu.make_async_copy(wd_h.at[layer], WD.at[at.q, pl.ds(at.c * 7, 7)], own.at[TILES]).wait()
 
 
 def gathers(at, WGU, WD, sgu, rgu, sd, rd):
@@ -138,34 +144,43 @@
 
 def forward_kernel(
     x_h, wg_h, wu_h, wd_h,
-    gu_o, a0t_o, h1_o, a1_o, a1t_o, wd_o,
-    WGU, WD, X, A, AT, MID, ST, ACC,
-    load, own, stage, out, sgu, rgu, sd, rd,
+    gu_o, a0t_o, h1_o, a1_o, a1t_o, wd_o, wgu1_o, wd1_o,
+    WGU, WD, X, A, AT, MID, ST, ACC, WGU1, WD1,
+    load, own, stage, out, done, sgu, rgu, sd, rd, own1, sgu1, rgu1, sd1, rd1,
 ):
     at = Place()
-    load_own(at, 0, wg_h, wu_h, wd_h, WGU, WD, own)
+    for j in range(TILES):
+        load_tile(at, 0, j, wg_h, wu_h, WGU.at[j], own.at[j])
+    own_down(at, 0, wd_h, WD, own).start()
+    load_tile(at, 1, 0, wg_h, wu_h, WGU1.at[0], own1.at[0])
+    down1_in = pltpu.make_async_copy(wd_h.at[1, pl.ds(0, AHEAD)], WD1.at[at.q, at.c], own1.at[1])
+    down1_in.start()
     x_in = pltpu.make_async_copy(x_h, X, load)
     x_in.start()
     barrier(at)
     gu, down = gathers(at, WGU, WD, sgu, rgu, sd, rd)
-
-    def start_tile(n, _):
+    gu1 = Gather(at, lambda n, s: WGU1.at[n, :, s], sgu1, rgu1)
+    down1 = Gather(at, lambda n, s: WD1.at[s // 2, s % 2, n], sd1, rd1)
+
+    def start_tile(n):
         wait_own_tile(at, n, WGU, own)
         gu.own(n)
-        return 0
-
-    lax.fori_loop(0, TILES, start_tile, 0)
-    wait_own_down(at, wd_h, 0, WD, own)
-    lax.fori_loop(0, TILES, lambda n, _: (down.own(n), 0)[1], 0)
+
+    loop(TILES, start_tile)
+    own_down(at, 0, wd_h, WD, own).wait()
+    loop(TILES, lambda n: down.own(n))
+    down1_in.wait()
+    loop(AHEAD, lambda n: down1.own(n))
+    wait_own_tile(at, 0, WGU1, own1)
+    gu1.own(0)
     x_in.wait()
 
-    def norm(m, _):
+    def norm(m):
         a = normed(X[block(m), :])
         A[block(m), :] = a
         AT[:, :, block(m)] = a.T.reshape(2, 448, ROWS)
-        return 0
-
-    lax.fori_loop(0, BLOCKS, norm, 0)
+
+    loop(BLOCKS, norm)
     a0t_out = pltpu.make_async_copy(AT, a0t_o, out.at[0])
     a0t_out.start()
     gu.first(0)
@@ -175,13 +190,16 @@
     def staged(j, m, slot):
         return pltpu.make_async_copy(ST.at[slot], gu_o.at[j, :, block(m), :], stage.at[slot])
 
-    def tile(j, _):
+    def tile(j):
         gu.whole(j)
-        pl.when(j < TILES - 2)(lambda: gu.first(j + 2))
-        pl.when(j >= TILES - 2)(lambda: down.first(j - TILES + 2))
-
-        def rows(m, _):
-            @pl.when(m == 2)
+
+        def rows(m):
+            @pl.when(m == 1)
+            def _():
+                pl.when(j < TILES - 2)(lambda: gu.first(j + 2))
+                pl.when(j >= TILES - 2)(lambda: down.first(j - TILES + 2))
+
+            @pl.when(m == 3)
             def _():
                 pl.when(j < TILES - 1)(lambda: gu.second(j + 1))
                 pl.when(j == TILES - 1)(lambda: down.second(0))
@@ -195,56 +213,86 @@
             ST[slot, 1] = up
             staged(j, m, slot).start()
             MID[j, block(m), :] = (gate * jax.nn.sigmoid(gate) * up).astype(BF16)
-            return 0
-
-        return lax.fori_loop(0, BLOCKS, rows, 0)
-
-    lax.fori_loop(0, TILES, tile, 0)
+
+        loop(BLOCKS, rows)
+
+    loop(TILES, tile)
     down.whole(0)
     down.first(2)
     down.second(1)
 
-    def below(j, _):
+    def below(j):
         down.whole(j + 1)
         pl.when(j < TILES - 3)(lambda: down.first(j + 3))
 
-        def rows(m, _):
+        def rows(m):
             pl.when((m == 2) & (j < TILES - 2))(lambda: down.second(j + 2))
+
+            @pl.when((m == 2) & (j >= TILES - 3))
+            def _():
+                pl.when(j == TILES - 3)(lambda: down1.first(0))
+                pl.when(j == TILES - 2)(lambda: down1.first(1))
+
             part = dot(MID[j, block(m), :], down_tile(WD, j))
             ACC[block(m), :] += part
-            return 0
-
-        return lax.fori_loop(0, BLOCKS, rows, 0)
+
+        loop(BLOCKS, rows)
 
     ACC[...] = jnp.zeros_like(ACC)
-    lax.fori_loop(0, TILES - 1, below, 0)
+    loop(TILES - 1, below)
     wd_out = pltpu.make_async_copy(WD, wd_o, out.at[1])
     wd_out.start()
     a0t_out.wait()
 
-    def finish(m, _):
+    gu1.first(0)
+    down1.second(0)
+
+    def finish(m):
+        @pl.when(m == 2)
+        def _():
+            down1.second(1)
+            gu1.second(0)
+
         total = ACC[block(m), :] + dot(MID[TILES - 1, block(m), :], down_tile(WD, TILES - 1))
         h = added(X[block(m), :], total.astype(BF16))
         X[block(m), :] = h
         a = normed(h)
         A[block(m), :] = a
         AT[:, :, block(m)] = a.T.reshape(2, 448, ROWS)
-        return 0
-
-    lax.fori_loop(0, BLOCKS, finish, 0)
-    outs = [pltpu.make_async_copy(v, o, out.at[2 + k]) for k, (v, o) in enumerate(((X, h1_o), (A, a1_o), (AT, a1t_o)))]
+        for one in block_out(m):
+            one.start()
+
+    def block_out(m):
+        return [
+            pltpu.make_async_copy(X.at[block(m), :], h1_o.at[block(m), :], done.at[0, m]),
+            pltpu.make_async_copy(A.at[block(m), :], a1_o.at[block(m), :], done.at[1, m]),
+            pltpu.make_async_copy(AT.at[:, :, block(m)], a1t_o.at[:, :, block(m)], done.at[2, m]),
+        ]
+
+    loop(BLOCKS, finish)
+    gu1.whole(0)
+    loop(AHEAD, lambda n: down1.whole(n))
+    pairs = ((WGU1, wgu1_o), (WD1, wd1_o))
+    outs = [pltpu.make_async_copy(v, o, out.at[2 + k]) for k, (v, o) in enumerate(pairs)]
     for o in outs:
         o.start()
     for slot in range(2):
         staged(TILES - 1, slot, slot).wait()
 
-    def sent(n, _):
+    def sent(n):
         gu.sent(n)
         down.sent(n)
-        return 0
-
-    lax.fori_loop(0, TILES, sent, 0)
+
+    loop(TILES, sent)
+    gu1.sent(0)
+    loop(AHEAD, lambda n: down1.sent(n))
     wd_out.wait()
+
+    def blocks_left(m):
+        for one in block_out(m):
+            one.wait()
+
+    loop(BLOCKS, blocks_left)
     for o in outs:
         o.wait()
 
@@ -254,7 +302,7 @@
 
 
 def backward_kernel(
-    a1_h, a1t_h, h1_h, dy_h, a0t_h, gu_h, wd0_h, wg_h, wu_h, wd_h,
+    a1_h, a1t_h, h1_h, dy_h, a0t_h, gu_h, wd0_h, wgu1_h, wd1_h, wg_h, wu_h, wd_h,
     gg_o, gu_o, gd_o, sq_o,
     WGU, WD, A, AT, DY, ACC, MID, DG, DU, TW, TD, RW, RD, FW, FD, BW, BD, ZW, ZD, OW, OD, SQW, SQD, SQ,
     load, own, gus, sgu, rgu, sd, rd, pair_s, pair_r, first_s, first_r, second_s, second_r, z_s, z_r, ow_s, od_s, od_remote_s, od_r, sq_s, sq_r,
@@ -262,8 +310,12 @@
 ):
     at = Place()
     c, q, qx, qy, qd = at.c, at.q, at.qx, at.qy, at.qd
-    load_own(at, 1, wg_h, wu_h, wd_h, WGU, WD, own)
-    loads = [pltpu.make_async_copy(h, v, load.at[k]) for k, (h, v) in enumerate(((a1_h, A), (a1t_h, AT), (dy_h, DY)))]
+    own_down(at, 1, wd_h, WD, own).start()
+    for j in range(1, TILES):
+        load_tile(at, 1, j, wg_h, wu_h, WGU.at[j], own.at[j])
+    pairs = [(a1_h, A), (wgu1_h.at[0], WGU.at[0]), (dy_h, DY), (a1t_h, AT)]
+    pairs += [(wd1_h.at[:, core], WD.at[:, pl.ds(7 * core, AHEAD)]) for core in range(2)]
+    loads = [pltpu.make_async_copy(h, v, load.at[k]) for k, (h, v) in enumerate(pairs)]
     for one in loads:
         one.start()
     h1_in = pltpu.make_async_copy(h1_h, A, load.at[0])
@@ -271,26 +323,19 @@
     a0t_in = pltpu.make_async_copy(a0t_h, AT, load.at[1])
     barrier(at)
     gather, down = gathers(at, WGU, WD, sgu, rgu, sd, rd)
-    wait_own_down(at, wd_h, 1, WD, own)
-    down.own(0)
-
-    def start_tile(j, _):
-        pl.when(j < TILES - 1)(lambda: down.own(j + 1))
-        wait_own_tile(at, j, WGU, own)
-        gather.own(j)
-        return 0
-
-    lax.fori_loop(0, TILES, start_tile, 0)
+    own_down(at, 1, wd_h, WD, own).wait()
+
+    def start_tile(j):
+        down.own(j + 2)
+        wait_own_tile(at, j + 1, WGU, own)
+        gather.own(j + 1)
+
+    loop(TILES - AHEAD, start_tile)
+    wait_own_tile(at, TILES - 1, WGU, own)
+    gather.own(TILES - 1)
     SQW[...] = jnp.zeros_like(SQW)
     SQD[...] = jnp.zeros_like(SQD)
     ACC[...] = jnp.zeros_like(ACC)
-    down.first(0)
-    down.first(1)
-    down.second(0)
-    gather.first(0)
-    down.second(1)
-    down.whole(0)
-    gather.second(0)
     for one in loads:
         one.wait()
 
@@ -316,12 +361,12 @@
 
     def first_copies(t, part):
         mine, into, _ = buffers(t, part)
-        to, near = ways(part)[0]
+        (to, near), _ = ways(part)
         return [remote(mine(p), into(n), first_s.at[2 * part + n, t % 2], first_r.at[2 * part + n, t % 2], to) for n, p in enumerate((near, qd))]
 
     def second_copy(t, part):
         mine, _, into = buffers(t, part)
-        to, near = ways(part)[1]
+        _, (to, near) = ways(part)
         return remote(mine(near), into, second_s.at[part, t % 2], second_r.at[part, t % 2], to)
 
     def z_copy(t, one):
@@ -343,24 +388,20 @@
 
     PARTS = ((0,), (1,), (2, 3))
 
-    def stage_one(t):
+    def stage_one(t, one):
         k, j = t % SLOTS, t % 2
-        spend(t, first_x, first_y)
-        for one in range(3):
-            pair_copy(t, one).wait()
-
-            def chip(p, _):
-                if one < 2:
-                    TW[k, one, p, c] = added(TW[k, one, p, c], RW[j, one, p])
-                else:
-                    TD[k, p, c] = added(TD[k, p, c], RD[j, p])
-                return 0
-
-            lax.fori_loop(0, 4, chip, 0)
-            for part in PARTS[one]:
-                for copy in first_copies(t, part):
-                    copy.start()
-        free(t, (pair_free, at.to_c))
+        pair_copy(t, one).wait()
+
+        def chip(p):
+            if one < 2:
+                TW[k, one, p, c] = added(TW[k, one, p, c], RW[j, one, p])
+            else:
+                TD[k, p, c] = added(TD[k, p, c], RD[j, p])
+
+        loop(4, chip)
+        for part in PARTS[one]:
+            for copy in first_copies(t, part):
+                copy.start()
 
     def stage_two(t):
         spend(t, second_x, second_y)
@@ -368,7 +409,7 @@
             for copy in first_copies(t, part):
                 copy.wait()
             mine, into, _ = buffers(t, part)
-            other = ways(part)[1][1]
+            _, (_, other) = ways(part)
             mine(other)[...] = added(mine(other)[...], into(1)[...])
             second_copy(t, part).start()
             mine(q)[...] = added(mine(q)[...], into(0)[...])
@@ -386,7 +427,7 @@
 
     def half(t, core):
         number = tile_of(t % TILES) * 2 + core
-        return number // 7, number % 7
+        return number // 7, pl.ds(pl.multiple_of(number % 7 * 64, 64), 64)
 
     def layer_of(t):
         return 1 - t // TILES
@@ -447,10 +488,10 @@
             ref[block(m), :] = value
 
     def layer_one(i):
-        pl.when(i < TILES - 1)(lambda: down.whole(i + 1))
-        gather.whole(i)
-
-        def rows(m, _):
+        pl.when((i > 0) & (i < TILES - 1))(lambda: down.whole(i + 1))
+        pl.when(i > 0)(lambda: gather.whole(i))
+
+        def rows(m):
             @pl.when((m == 2) & (i < TILES - 1))
             def _():
                 pl.when(i < TILES - 2)(lambda: down.first(i + 2))
@@ -463,9 +504,8 @@
             values = between(gate, up, by_mid)
             store_between(m, values)
             ACC[block(m), :] += dot(values[1], gate_up(WGU, i, 0), (1, 1)) + dot(values[2], gate_up(WGU, i, 1), (1, 1))
-            return 0
-
-        lax.fori_loop(0, BLOCKS, rows, 0)
+
+        loop(BLOCKS, rows)
 
     def kept(n):
         i, m, slot = n // BLOCKS, n % BLOCKS, n % 2
@@ -481,22 +521,21 @@
         h1_in.wait()
         wd0_in.wait()
 
-        def rows(m, _):
+        def rows(m):
             wide = A[block(m), :].astype(F32)
             by_a = ACC[block(m), :].astype(BF16).astype(F32)
             scale = lax.rsqrt(jnp.mean(wide**2, -1, keepdims=True) + 1e-6)
             along = jnp.mean(by_a * wide, -1, keepdims=True) * scale * scale
             by_h = (scale * (by_a - wide * along)).astype(BF16)
             DY[block(m), :] = added(DY[block(m), :], by_h)
-            return 0
-
-        lax.fori_loop(0, BLOCKS, rows, 0)
+
+        loop(BLOCKS, rows)
         for one in kept(0):
             one.start()
         a0t_in.wait()
 
     def layer_zero(i):
-        def rows(m, _):
+        def rows(m):
             n = i * BLOCKS + m
             slot = n % 2
 
@@ -510,31 +549,36 @@
             gate, up = (ACC[pl.ds(pl.multiple_of(slot * 1024 + which * 512, 512), 512), pl.ds(0, 512)] for which in range(2))
             by_mid = dot(DY[block(m), :], down_tile(WD, i), (1, 1)).astype(BF16).astype(F32)
             store_between(m, between(gate, up, by_mid))
-            return 0
-
-        lax.fori_loop(0, BLOCKS, rows, 0)
+
+        loop(BLOCKS, rows)
 
     def gradients(t):
         k = t % SLOTS
         spend(t, pair_free)
         for which, by in enumerate((DG, DU)):
 
-            def rows(half, _):
+            def rows(half):
                 TW[k, which, pl.ds(2 * half, 2)] = dot(AT[half], by[...]).astype(BF16).reshape(2, 2, 112, WIDE)
-                return 0
-
-            lax.fori_loop(0, 2, rows, 0)
+
+            loop(2, rows)
             pair_copy(t, which).start()
         TD[k] = dot(MID[...], DY[...], (0, 0)).astype(BF16).reshape(4, 2, 64, D)
         pair_copy(t, 2).start()
 
-    def step(t, _):
+    def step(t):
         pl.when(t < TILES)(lambda: layer_one(t))
         pl.when(t == TILES)(turn)
         pl.when((t >= TILES) & (t < STEPS))(lambda: layer_zero(t - TILES))
-        pl.when((t >= 1) & (t <= STEPS))(lambda: stage_one(t - 1))
+
+        @pl.when((t >= 1) & (t <= STEPS))
+        def _():
+            spend(t - 1, first_x, first_y)
+            for one in range(3):
+                stage_one(t - 1, one)
+            free(t - 1, (pair_free, at.to_c))
+
+        pl.when((t >= 3) & (t <= STEPS + 2))(lambda: stage_three(t - 3))
         pl.when((t >= 2) & (t <= STEPS + 1))(lambda: stage_two(t - 2))
-        pl.when((t >= 3) & (t <= STEPS + 2))(lambda: stage_three(t - 3))
         pl.when(t >= 4)(lambda: stage_four(t - 4))
 
         @pl.when(t < TILES - 1)
@@ -545,13 +589,12 @@
         @pl.when(t == TILES - 1)
         def _():
             h1_in.start()
-            lax.fori_loop(0, TILES, lambda n, _: (down.sent(n), 0)[1], 0)
+            loop(TILES - AHEAD, lambda n: down.sent(n + AHEAD))
             wd0_in.start()
 
         pl.when(t < STEPS)(lambda: gradients(t))
-        return 0
-
-    lax.fori_loop(0, STEPS + 4, step, 0)
+
+    loop(STEPS + 4, step)
 
     mine = jnp.sum(SQW[...], keepdims=True) + jnp.sum(SQD[...], keepdims=True)
     SQ[at.s] = jnp.broadcast_to(mine, (8, 128))
@@ -564,14 +607,13 @@
     out_wait(STEPS - 2)
     out_wait(STEPS - 1)
 
-    lax.fori_loop(0, TILES, lambda n, _: (gather.sent(n), 0)[1], 0)
-
-    def arrived(t, _):
+    loop(TILES - 1, lambda n: gather.sent(n + 1))
+
+    def arrived(t):
         owner, _ = half(t, 1 - c)
         pl.when(owner == c)(lambda: down_remote(t, 1 - c).wait_recv())
-        return 0
-
-    lax.fori_loop(0, STEPS, arrived, 0)
+
+    loop(STEPS, arrived)
     for n in range(1, 8):
         square(n, (at.s + 8 - n) % 8).wait_recv()
         square(n, at.s).wait_send()
@@ -598,27 +640,29 @@
         name="forward",
         out_shape=[
             shape((TILES, 2, T, WIDE), F32), shape((2, 448, T)), shape((T, D)), shape((T, D)), shape((2, 448, T)), shape((4, 14, 64, D)),
+            shape((1, 2, 8, 112, WIDE)), shape((4, 2, AHEAD, 64, D)),
         ],
         in_specs=[ANY] * 4,
-        out_specs=[ANY] * 6,
+        out_specs=[ANY] * 8,
         scratch_shapes=[
             pltpu.VMEM((TILES, 2, 8, 112, WIDE), BF16), pltpu.VMEM((4, 14, 64, D), BF16), pltpu.VMEM((T, D), BF16), pltpu.VMEM((T, D), BF16),
             pltpu.VMEM((2, 448, T), BF16), pltpu.VMEM((TILES, T, WIDE), BF16), pltpu.VMEM((2, 2, ROWS, WIDE), F32), pltpu.VMEM((T, D), F32),
-            pltpu.SemaphoreType.DMA, sems(TILES + 1), sems(2), sems(5), *GATHER_SEMS,
+            pltpu.VMEM((1, 2, 8, 112, WIDE), BF16), pltpu.VMEM((4, 2, AHEAD, 64, D), BF16),
+            pltpu.SemaphoreType.DMA, sems(TILES + 1), sems(2), sems(4), sems(3, BLOCKS), *GATHER_SEMS, sems(2), *[sems(7, 1)] * 2, *[sems(7, AHEAD)] * 2,
         ],
         compiler_params=pltpu.CompilerParams(collective_id=0, has_side_effects=True, vmem_limit_bytes=VMEM_LIMIT),
     )(x, w_gate, w_up, w_down)
 
 
-def backward(a1, a1t, h1, dy, a0t, gu, wd0, w_gate, w_up, w_down):
+def backward(a1, a1t, h1, dy, a0t, gu, wd0, *shards):
     pair = ((2, 2, 4, 112, WIDE), (2, 4, 64, D))
     two = ((2, 2, 2, 112, WIDE), (2, 2, 64, D))
     one = ((2, 2, 112, WIDE), (2, 64, D))
     return pl.pallas_call(
         backward_kernel,
         name="backward",
-        out_shape=[shape((2, 112, FF)), shape((2, 112, FF)), shape((2, 7, 64, D)), shape((8, 128), F32)],
-        in_specs=[ANY] * 10,
+        out_shape=[shape((2, 112, FF)), shape((2, 112, FF)), shape((2, 448, D)), shape((8, 128), F32)],
+        in_specs=[ANY] * 12,
         out_specs=[ANY] * 3 + [pl.BlockSpec(memory_space=pltpu.VMEM)],
         scratch_shapes=[
             pltpu.VMEM((TILES, 2, 8, 112, WIDE), BF16), pltpu.VMEM((4, 14, 64, D), BF16), pltpu.VMEM((T, D), BF16), pltpu.VMEM((2, 448, T), BF16),
@@ -626,13 +670,13 @@
             pltpu.VMEM((SLOTS, 2, 4, 2, 112, WIDE), BF16), pltpu.VMEM((SLOTS, 4, 2, 64, D), BF16),
             *[pltpu.VMEM(dims, BF16) for dims in (*pair, *two, *one, *one, *one)],
             pltpu.VMEM((8, WIDE), F32), pltpu.VMEM((8, D), F32), pltpu.VMEM((8, 8, 128), F32),
-            sems(3), sems(TILES + 1), sems(2, 2), *GATHER_SEMS,
+            sems(6), sems(TILES + 1), sems(2, 2), *GATHER_SEMS,
             sems(3, 2), sems(3, 2), sems(8, 2), sems(8, 2), sems(4, 2), sems(4, 2), sems(3, 2), sems(3, 2), sems(2), sems(2), sems(2), sems(STEPS),
             sems(7), sems(7),
             *[pltpu.SemaphoreType.REGULAR] * 6,
         ],
         compiler_params=pltpu.CompilerParams(collective_id=1, has_side_effects=True, vmem_limit_bytes=VMEM_LIMIT),
-    )(a1, a1t, h1, dy, a0t, gu, wd0, w_gate, w_up, w_down)
+    )(a1, a1t, h1, dy, a0t, gu, wd0, *shards)
 
 
 def adamw(w, m, v, g):
@@ -646,9 +690,8 @@
     def step(x, dy, *arrays):
         weights, m, v = (arrays[i : i + 3] for i in (0, 3, 6))
         shards = (weights[0], weights[1], weights[2].reshape(2, 7, 64, D))
-        gu, a0t, h1, a1, a1t, wd0 = forward(x[0], *shards)
-        *gradients, squares = backward(a1, a1t, h1, dy[0], a0t, gu, wd0, *shards)
-        gradients[2] = gradients[2].reshape(2, 448, D)
+        gu, a0t, h1, a1, a1t, wd0, *ahead = forward(x[0], *shards)
+        *gradients, squares = backward(a1, a1t, h1, dy[0], a0t, gu, wd0, *ahead, *shards)
         count = mesh.shape["s"] * sum(g.size for g in gradients)
         factor = jnp.minimum(1.0, 0.5 * lax.rsqrt(squares[0, 0] / count + 1e-30))
         new = [adamw(w.astype(F32), m, v, g.astype(F32) * factor) for w, m, v, g in zip(weights, m, v, gradients, strict=True)]

time: 418 us -> 401 us (0.959)
  Pallas kernels: 397 us -> 379 us
  local copies, waits for them, and re-layouts: 1.38 us -> 5.96 us
    pallas_call x1, Pallas kernels: 308 us -> 283 us  [backward(): pl.pallas_call(backward_kernel, name='backward', out_shape=[shape((2, 112...]
    pallas_call x1, Pallas kernels: 89.1 us -> 95.9 us  [forward(): pl.pallas_call(forward_kernel, name='forward', out_shape=[shape((TILES, 2...]
    unnamed x12 -> x14, local copies, waits for them, and re-layouts: 0.04 us -> 4.77 us
where the time goes in v3:
time: 401 us
  Pallas kernels  379 us (95%)
  other arithmetic  14.8 us (4%)
  local copies, waits for them, and re-layouts  5.96 us (1%)
    pallas_call x1, Pallas kernels, backward(): pl.pallas_call(backward_kernel, name='backward', out_shape=[shape((2, 112...  283 us
    pallas_call x1, Pallas kernels, forward(): pl.pallas_call(forward_kernel, name='forward', out_shape=[shape((TILES, 2...  95.9 us
    convert_element_type x2, other arithmetic, adamw(): return ((w - 0.02 * step).astype(BF16), m, v)  14.8 us

profile of v3, /device:TPU:0, one launch (start us, length us, event | category | flops | bytes accessed | tf_op | source)
XLA Modules:
  0.0 400.6 jit_solution(9022536521435728220)
XLA Ops:
  0.6 95.9 %forward.1 = (f32[7,2,2048,512]{3,2,1,0:T(8,128)}, bf16[2,448,2048]{2,1,0:T(8,128)(2,1)}, bf16[2048,896]{1,0:T(8,128)(2,1)}, bf16[2048,896]{1,0:T(8,128)(2,1)}, ...) custom-call(bf16[2048,896]{1,0:T(8,128)(2,1)} %bitcast.6, ...), custom_call_target="tpu_custom_call" | custom-call | tf_op jit(solution)/shard_map/forward/pallas_call | solution.py:638
  96.5 282.6 %backward.1 = (bf16[2,112,3584]{2,1,0:T(8,128)(2,1)}, bf16[2,112,3584]{2,1,0:T(8,128)(2,1)}, bf16[2,448,896]{2,1,0:T(8,128)(2,1)}, f32[8,128]{1,0:T(8,128)}) custom-call(bf16[2048,896]{1,0:T(8,128)(2,1)} %get-tuple-element.21.a1_h, bf16[2,448,2048]{2,1,0:T(8,128)(2,1)} %get-tuple-element.22.a1t_h, bf16[2048,896]{1,0:T(8,128)(2,1)} %get-tuple-element.23.h1_h, ...), custom_call_target="tpu_custom_call" | custom-call | tf_op jit(solution)/shard_map/backward/pallas_call | solution.py:661
  379.2 1.2 slice.3
  381.0 0.0 copy-start
  381.1 0.0 copy-start.1
  381.1 0.0 copy-start.2
  381.1 0.0 copy-start.3
  381.1 0.0 copy-start.4
  381.1 0.0 copy-start.5
  381.1 0.0 copy-start.6
  381.1 6.9 %fusion.8 = (bf16[2,448,896]{2,1,0:T(8,128)(2,1)}, f32[2,448,896]{2,1,0:T(8,128)}, f32[2,448,896]{2,1,0:T(8,128)}) fusion(bf16[2,448,896]{2,1,0:T(8,128)(2,1)} %param.15, f32[]{:T(128)} %bitcast.3, bf16[2,448,896]{2,1,0:T(8,128)(2,1)} %get-tuple-element.32, f32[2,448,896]{2,1,0:T(8,128)} %param.21, f32[2,448,896]{2,1,0:T(8,128)} %param.18), kind=kLoop, calls=%fused_computation.17 | loop fusion | flops 13647872 | bytes 17661956 | tf_op jit(solution)/shard_map/convert_element_type | solution.py:686
  388.0 0.0 copy-done
  388.0 0.0 copy-done.1
  388.0 1.6 copy-done.2
  389.6 0.9 copy-done.3
  390.5 0.9 copy-done.4
  391.4 0.9 copy-done.5
  392.4 0.4 copy-done.6
  392.8 7.9 %fusion.2 = (bf16[2,112,3584]{2,1,0:T(8,128)(2,1)}, f32[2,112,3584]{2,1,0:T(8,128)}, f32[2,112,3584]{2,1,0:T(8,128)}, bf16[2,112,3584]{2,1,0:T(8,128)(2,1)}, f32...) fusion(bf16[2,112,3584]{2,1,0:T(8,128)(2,1)S(1)} %copy-done, f32[]{:T(128)} %bitcast.3, ...), kind=kLoop, calls=%fused_computation.11 | loop fusion | flops 27295744 | bytes 35323908 | tf_op jit(solution)/shard_map/convert_element_type | solution.py:686
Async XLA Ops:
  381.0 7.0 %copy-start = (bf16[2,112,3584]{2,1,0:T(8,128)(2,1)S(1)}, bf16[2,112,3584]{2,1,0:T(8,128)(2,1)}, u32[]{:S(2)}) copy-start(bf16[2,112,3584]{2,1,0:T(8,128)(2,1)} %wg_h.3) | copy-start | bytes 4816900
  381.1 7.0 %copy-start.1 = (bf16[2,112,3584]{2,1,0:T(8,128)(2,1)S(1)}, bf16[2,112,3584]{2,1,0:T(8,128)(2,1)}, u32[]{:S(2)}) copy-start(bf16[2,112,3584]{2,1,0:T(8,128)(2,1)} %wu_h.3) | copy-start | bytes 4816900
  381.1 8.5 %copy-start.2 = (f32[2,112,3584]{2,1,0:T(8,128)S(1)}, f32[2,112,3584]{2,1,0:T(8,128)}, u32[]{:S(2)}) copy-start(f32[2,112,3584]{2,1,0:T(8,128)} %param.19) | copy-start | bytes 9633796
  381.1 9.4 %copy-start.3 = (f32[2,112,3584]{2,1,0:T(8,128)S(1)}, f32[2,112,3584]{2,1,0:T(8,128)}, u32[]{:S(2)}) copy-start(f32[2,112,3584]{2,1,0:T(8,128)} %param.16) | copy-start | bytes 9633796
  381.1 10.3 %copy-start.4 = (f32[2,112,3584]{2,1,0:T(8,128)S(1)}, f32[2,112,3584]{2,1,0:T(8,128)}, u32[]{:S(2)}) copy-start(f32[2,112,3584]{2,1,0:T(8,128)} %param.20) | copy-start | bytes 9633796
  381.1 11.2 %copy-start.5 = (f32[2,112,3584]{2,1,0:T(8,128)S(1)}, f32[2,112,3584]{2,1,0:T(8,128)}, u32[]{:S(2)}) copy-start(f32[2,112,3584]{2,1,0:T(8,128)} %param.17) | copy-start | bytes 9633796
  381.1 11.7 %copy-start.6 = (bf16[2,112,3584]{2,1,0:T(8,128)(2,1)S(1)}, bf16[2,112,3584]{2,1,0:T(8,128)(2,1)}, u32[]{:S(2)}) copy-start(bf16[2,112,3584]{2,1,0:T(8,128)(2,1)} %get-tuple-element.29) | copy-start | bytes 4816900

commit v4 on v3

--- a/solution.py
+++ b/solution.py
@@ -12,6 +12,7 @@
 STEPS = 2 * TILES
 AHEAD = 2
 SLOTS = 4
+OTHERS = range(1, 8)
 F32, BF16 = jnp.float32, jnp.bfloat16
 VMEM_LIMIT = 67_043_328
 ANY = pl.BlockSpec(memory_space=pl.ANY)
@@ -33,6 +34,12 @@
     wide = h.astype(F32)
     scale = lax.rsqrt(jnp.mean(wide**2, -1, keepdims=True) + 1e-6)
     return (wide * scale).astype(BF16)
+
+
+def by_owner(AT, m, a):
+    turned = a.T.reshape(4, 2, 112, ROWS)
+    for core in range(2):
+        AT[core, :, block(m)] = turned[:, core].reshape(448, ROWS)
 
 
 def block(i):
@@ -64,7 +71,7 @@
 
 def barrier(at):
     sem = pltpu.get_barrier_semaphore()
-    partners = [at.plane(n) for n in range(1, 8)] + [at.to_z]
+    partners = [at.plane(n) for n in OTHERS] + [at.to_z]
     for to in partners:
         pl.semaphore_signal(sem, inc=1, device_id=to, device_id_type=MESH)
     pl.semaphore_wait(sem, len(partners))
@@ -178,7 +185,7 @@
     def norm(m):
         a = normed(X[block(m), :])
         A[block(m), :] = a
-        AT[:, :, block(m)] = a.T.reshape(2, 448, ROWS)
+        by_owner(AT, m, a)
 
     loop(BLOCKS, norm)
     a0t_out = pltpu.make_async_copy(AT, a0t_o, out.at[0])
@@ -258,7 +265,7 @@
         X[block(m), :] = h
         a = normed(h)
         A[block(m), :] = a
-        AT[:, :, block(m)] = a.T.reshape(2, 448, ROWS)
+        by_owner(AT, m, a)
         for one in block_out(m):
             one.start()
 
@@ -304,7 +311,7 @@
 def backward_kernel(
     a1_h, a1t_h, h1_h, dy_h, a0t_h, gu_h, wd0_h, wgu1_h, wd1_h, wg_h, wu_h, wd_h,
     gg_o, gu_o, gd_o, sq_o,
-    WGU, WD, A, AT, DY, ACC, MID, DG, DU, TW, TD, RW, RD, FW, FD, BW, BD, ZW, ZD, OW, OD, SQW, SQD, SQ,
+    WGU, WD, A, AT, DY, ACC, MID, DG, DU, TS, TW, TD, RW, RD, FW, FD, BW, BD, ZW, ZD, OW, OD, SQW, SQD, SQ,
     load, own, gus, sgu, rgu, sd, rd, pair_s, pair_r, first_s, first_r, second_s, second_r, z_s, z_r, ow_s, od_s, od_remote_s, od_r, sq_s, sq_r,
     pair_free, first_x, first_y, second_x, second_y, z_free,
 ):
@@ -313,14 +320,15 @@
     own_down(at, 1, wd_h, WD, own).start()
     for j in range(1, TILES):
         load_tile(at, 1, j, wg_h, wu_h, WGU.at[j], own.at[j])
-    pairs = [(a1_h, A), (wgu1_h.at[0], WGU.at[0]), (dy_h, DY), (a1t_h, AT)]
+    pairs = [(a1_h, A), (wgu1_h.at[0], WGU.at[0])]
     pairs += [(wd1_h.at[:, core], WD.at[:, pl.ds(7 * core, AHEAD)]) for core in range(2)]
+    pairs += [(dy_h, DY), (a1t_h, AT)]
     loads = [pltpu.make_async_copy(h, v, load.at[k]) for k, (h, v) in enumerate(pairs)]
     for one in loads:
         one.start()
     h1_in = pltpu.make_async_copy(h1_h, A, load.at[0])
     wd0_in = pltpu.make_async_copy(wd0_h, WD, load.at[2])
-    a0t_in = pltpu.make_async_copy(a0t_h, AT, load.at[1])
+    a0t_in = pltpu.make_async_copy(a0t_h, AT, load.at[3])
     barrier(at)
     gather, down = gathers(at, WGU, WD, sgu, rgu, sd, rd)
     own_down(at, 1, wd_h, WD, own).wait()
@@ -336,6 +344,7 @@
     SQW[...] = jnp.zeros_like(SQW)
     SQD[...] = jnp.zeros_like(SQD)
     ACC[...] = jnp.zeros_like(ACC)
+    at_in = loads.pop()
     for one in loads:
         one.wait()
 
@@ -344,13 +353,13 @@
 
     def pair_copy(t, one):
         k, j = t % SLOTS, t % 2
-        src, dst = (TW.at[k, one, :, 1 - c], RW.at[j, one]) if one < 2 else (TD.at[k, :, 1 - c], RD.at[j])
+        src, dst = (TS.at[one], RW.at[j, one]) if one < 2 else (TD.at[k, :, 1 - c], RD.at[j])
         return remote(src, dst, pair_s.at[one, j], pair_r.at[one, j], at.to_c)
 
     def buffers(t, part):
         k, j = t % SLOTS, t % 2
         if part < 2:
-            return (lambda p: TW.at[k, part, p, c]), (lambda n: FW.at[j, part, n]), BW.at[j, part]
+            return (lambda p: TW.at[k, part, p]), (lambda n: FW.at[j, part, n]), BW.at[j, part]
         rows = pl.ds(32 * (part - 2), 32)
         return (lambda p: TD.at[k, p, c, rows]), (lambda n: FD.at[j, n, rows]), BD.at[j, rows]
 
@@ -371,7 +380,7 @@
 
     def z_copy(t, one):
         k, j = t % SLOTS, t % 2
-        src, dst = (TW.at[k, one, q, c], ZW.at[j, one]) if one < 2 else (TD.at[k, q, c], ZD.at[j])
+        src, dst = (TW.at[k, one, q], ZW.at[j, one]) if one < 2 else (TD.at[k, q, c], ZD.at[j])
         return remote(src, dst, z_s.at[one, j], z_r.at[one, j], at.to_z)
 
     def spend(t, *sems):
@@ -388,20 +397,21 @@
 
     PARTS = ((0,), (1,), (2, 3))
 
-    def stage_one(t, one):
-        k, j = t % SLOTS, t % 2
-        pair_copy(t, one).wait()
-
-        def chip(p):
-            if one < 2:
-                TW[k, one, p, c] = added(TW[k, one, p, c], RW[j, one, p])
-            else:
-                TD[k, p, c] = added(TD[k, p, c], RD[j, p])
-
-        loop(4, chip)
+    def first_start(t, one):
         for part in PARTS[one]:
             for copy in first_copies(t, part):
                 copy.start()
+
+    def stage_one(t):
+        k, j = t % SLOTS, t % 2
+        pair_copy(t, 2).wait()
+
+        def chip(p):
+            TD[k, p, c] = added(TD[k, p, c], RD[j, p])
+
+        loop(4, chip)
+        first_start(t, 2)
+        free(t, (pair_free, at.to_c))
 
     def stage_two(t):
         spend(t, second_x, second_y)
@@ -466,7 +476,7 @@
         pl.when(t >= 2)(lambda: out_wait(t - 2))
         for one in range(3):
             z_copy(t, one).wait()
-            g = added(TW[k, one, q, c], ZW[j, one]) if one < 2 else added(TD[k, q, c], ZD[j])
+            g = added(TW[k, one, q], ZW[j, one]) if one < 2 else added(TD[k, q, c], ZD[j])
             wide = g.astype(F32)
             if one < 2:
                 OW[j, one] = g
@@ -532,7 +542,6 @@
         loop(BLOCKS, rows)
         for one in kept(0):
             one.start()
-        a0t_in.wait()
 
     def layer_zero(i):
         def rows(m):
@@ -553,30 +562,25 @@
         loop(BLOCKS, rows)
 
     def gradients(t):
-        k = t % SLOTS
+        k, j = t % SLOTS, t % 2
         spend(t, pair_free)
         for which, by in enumerate((DG, DU)):
-
-            def rows(half):
-                TW[k, which, pl.ds(2 * half, 2)] = dot(AT[half], by[...]).astype(BF16).reshape(2, 2, 112, WIDE)
-
-            loop(2, rows)
+            TS[which] = dot(AT[1 - c], by[...]).astype(BF16).reshape(4, 112, WIDE)
             pair_copy(t, which).start()
         TD[k] = dot(MID[...], DY[...], (0, 0)).astype(BF16).reshape(4, 2, 64, D)
         pair_copy(t, 2).start()
+        spend(t, first_x, first_y)
+        for which, by in enumerate((DG, DU)):
+            pair_copy(t, which).wait()
+            TW[k, which] = (dot(AT[c], by[...]).reshape(4, 112, WIDE) + RW[j, which].astype(F32)).astype(BF16)
+            first_start(t, which)
 
     def step(t):
         pl.when(t < TILES)(lambda: layer_one(t))
         pl.when(t == TILES)(turn)
         pl.when((t >= TILES) & (t < STEPS))(lambda: layer_zero(t - TILES))
 
-        @pl.when((t >= 1) & (t <= STEPS))
-        def _():
-            spend(t - 1, first_x, first_y)
-            for one in range(3):
-                stage_one(t - 1, one)
-            free(t - 1, (pair_free, at.to_c))
-
+        pl.when((t >= 1) & (t <= STEPS))(lambda: stage_one(t - 1))
         pl.when((t >= 3) & (t <= STEPS + 2))(lambda: stage_three(t - 3))
         pl.when((t >= 2) & (t <= STEPS + 1))(lambda: stage_two(t - 2))
         pl.when(t >= 4)(lambda: stage_four(t - 4))
@@ -592,6 +596,8 @@
             loop(TILES - AHEAD, lambda n: down.sent(n + AHEAD))
             wd0_in.start()
 
+        pl.when(t == 0)(at_in.wait)
+        pl.when(t == TILES)(a0t_in.wait)
         pl.when(t < STEPS)(lambda: gradients(t))
 
     loop(STEPS + 4, step)
@@ -602,7 +608,7 @@
     def square(n, from_):
         return remote(SQ.at[from_], SQ.at[from_], sq_s.at[n - 1], sq_r.at[n - 1], at.plane(n))
 
-    for n in range(1, 8):
+    for n in OTHERS:
         square(n, at.s).start()
     out_wait(STEPS - 2)
     out_wait(STEPS - 1)
@@ -614,11 +620,11 @@
         pl.when(owner == c)(lambda: down_remote(t, 1 - c).wait_recv())
 
     loop(STEPS, arrived)
-    for n in range(1, 8):
+    for n in OTHERS:
         square(n, (at.s + 8 - n) % 8).wait_recv()
         square(n, at.s).wait_send()
     total = SQ[0]
-    for n in range(1, 8):
+    for n in OTHERS:
         total += SQ[n]
     sq_o[...] = total
 
@@ -667,7 +673,7 @@
         scratch_shapes=[
             pltpu.VMEM((TILES, 2, 8, 112, WIDE), BF16), pltpu.VMEM((4, 14, 64, D), BF16), pltpu.VMEM((T, D), BF16), pltpu.VMEM((2, 448, T), BF16),
             pltpu.VMEM((T, D), BF16), pltpu.VMEM((T, D), F32), *[pltpu.VMEM((T, WIDE), BF16)] * 3,
-            pltpu.VMEM((SLOTS, 2, 4, 2, 112, WIDE), BF16), pltpu.VMEM((SLOTS, 4, 2, 64, D), BF16),
+            pltpu.VMEM((2, 4, 112, WIDE), BF16), pltpu.VMEM((SLOTS, 2, 4, 112, WIDE), BF16), pltpu.VMEM((SLOTS, 4, 2, 64, D), BF16),
             *[pltpu.VMEM(dims, BF16) for dims in (*pair, *two, *one, *one, *one)],
             pltpu.VMEM((8, WIDE), F32), pltpu.VMEM((8, D), F32), pltpu.VMEM((8, 8, 128), F32),
             sems(6), sems(TILES + 1), sems(2, 2), *GATHER_SEMS,

time: 401 us -> 398 us (level)
  no operation moved by 1% of the time
where the time goes in v4:
time: 398 us; the launch traced here: 397 us
  Pallas kernels  375 us (94%)
  other arithmetic  14.8 us (4%)
  local copies, waits for them, and re-layouts  5.96 us (1%)
    pallas_call x1, Pallas kernels, backward(): pl.pallas_call(backward_kernel, name='backward', out_shape=[shape((2, 112...  279 us
    pallas_call x1, Pallas kernels, forward(): pl.pallas_call(forward_kernel, name='forward', out_shape=[shape((TILES, 2...  95.9 us
    convert_element_type x2, other arithmetic, adamw(): return ((w - 0.02 * step).astype(BF16), m, v)  14.8 us

profile of v4, /device:TPU:0, one launch (start us, length us, event | category | flops | bytes accessed | tf_op | source)
XLA Modules:
  0.0 397.5 jit_solution(5166783874770688931)
XLA Ops:
  0.6 95.9 %forward.1 = (f32[7,2,2048,512]{3,2,1,0:T(8,128)}, bf16[2,448,2048]{2,1,0:T(8,128)(2,1)}, bf16[2048,896]{1,0:T(8,128)(2,1)}, bf16[2048,896]{1,0:T(8,128)(2,1)}, ...) custom-call(bf16[2048,896]{1,0:T(8,128)(2,1)} %bitcast.6, ...), custom_call_target="tpu_custom_call" | custom-call | tf_op jit(solution)/shard_map/forward/pallas_call | solution.py:644
  96.5 279.4 %backward.1 = (bf16[2,112,3584]{2,1,0:T(8,128)(2,1)}, bf16[2,112,3584]{2,1,0:T(8,128)(2,1)}, bf16[2,448,896]{2,1,0:T(8,128)(2,1)}, f32[8,128]{1,0:T(8,128)}) custom-call(bf16[2048,896]{1,0:T(8,128)(2,1)} %get-tuple-element.21.a1_h, bf16[2,448,2048]{2,1,0:T(8,128)(2,1)} %get-tuple-element.22.a1t_h, bf16[2048,896]{1,0:T(8,128)(2,1)} %get-tuple-element.23.h1_h, ...), custom_call_target="tpu_custom_call" | custom-call | tf_op jit(solution)/shard_map/backward/pallas_call | solution.py:667
  376.0 1.2 slice.3
  377.9 0.0 copy-start
  377.9 0.0 copy-start.1
  377.9 0.0 copy-start.2
  377.9 0.0 copy-start.3
  377.9 0.0 copy-start.4
  377.9 0.0 copy-start.5
  378.0 0.0 copy-start.6
  378.0 6.9 %fusion.8 = (bf16[2,448,896]{2,1,0:T(8,128)(2,1)}, f32[2,448,896]{2,1,0:T(8,128)}, f32[2,448,896]{2,1,0:T(8,128)}) fusion(bf16[2,448,896]{2,1,0:T(8,128)(2,1)} %param.15, f32[]{:T(128)} %bitcast.3, bf16[2,448,896]{2,1,0:T(8,128)(2,1)} %get-tuple-element.32, f32[2,448,896]{2,1,0:T(8,128)} %param.21, f32[2,448,896]{2,1,0:T(8,128)} %param.18), kind=kLoop, calls=%fused_computation.17 | loop fusion | flops 13647872 | bytes 17661956 | tf_op jit(solution)/shard_map/convert_element_type | solution.py:692
  384.9 0.0 copy-done
  384.9 0.0 copy-done.1
  384.9 1.6 copy-done.2
  386.4 0.9 copy-done.3
  387.4 0.9 copy-done.4
  388.3 0.9 copy-done.5
  389.2 0.4 copy-done.6
  389.6 7.9 %fusion.2 = (bf16[2,112,3584]{2,1,0:T(8,128)(2,1)}, f32[2,112,3584]{2,1,0:T(8,128)}, f32[2,112,3584]{2,1,0:T(8,128)}, bf16[2,112,3584]{2,1,0:T(8,128)(2,1)}, f32...) fusion(bf16[2,112,3584]{2,1,0:T(8,128)(2,1)S(1)} %copy-done, f32[]{:T(128)} %bitcast.3, ...), kind=kLoop, calls=%fused_computation.11 | loop fusion | flops 27295744 | bytes 35323908 | tf_op jit(solution)/shard_map/convert_element_type | solution.py:692
Async XLA Ops:
  377.9 7.0 %copy-start = (bf16[2,112,3584]{2,1,0:T(8,128)(2,1)S(1)}, bf16[2,112,3584]{2,1,0:T(8,128)(2,1)}, u32[]{:S(2)}) copy-start(bf16[2,112,3584]{2,1,0:T(8,128)(2,1)} %wg_h.3) | copy-start | bytes 4816900
  377.9 7.0 %copy-start.1 = (bf16[2,112,3584]{2,1,0:T(8,128)(2,1)S(1)}, bf16[2,112,3584]{2,1,0:T(8,128)(2,1)}, u32[]{:S(2)}) copy-start(bf16[2,112,3584]{2,1,0:T(8,128)(2,1)} %wu_h.3) | copy-start | bytes 4816900
  377.9 8.5 %copy-start.2 = (f32[2,112,3584]{2,1,0:T(8,128)S(1)}, f32[2,112,3584]{2,1,0:T(8,128)}, u32[]{:S(2)}) copy-start(f32[2,112,3584]{2,1,0:T(8,128)} %param.19) | copy-start | bytes 9633796
  377.9 9.4 %copy-start.3 = (f32[2,112,3584]{2,1,0:T(8,128)S(1)}, f32[2,112,3584]{2,1,0:T(8,128)}, u32[]{:S(2)}) copy-start(f32[2,112,3584]{2,1,0:T(8,128)} %param.16) | copy-start | bytes 9633796
  377.9 10.3 %copy-start.4 = (f32[2,112,3584]{2,1,0:T(8,128)S(1)}, f32[2,112,3584]{2,1,0:T(8,128)}, u32[]{:S(2)}) copy-start(f32[2,112,3584]{2,1,0:T(8,128)} %param.20) | copy-start | bytes 9633796
  377.9 11.2 %copy-start.5 = (f32[2,112,3584]{2,1,0:T(8,128)S(1)}, f32[2,112,3584]{2,1,0:T(8,128)}, u32[]{:S(2)}) copy-start(f32[2,112,3584]{2,1,0:T(8,128)} %param.17) | copy-start | bytes 9633796
  378.0 11.7 %copy-start.6 = (bf16[2,112,3584]{2,1,0:T(8,128)(2,1)S(1)}, bf16[2,112,3584]{2,1,0:T(8,128)(2,1)}, u32[]{:S(2)}) copy-start(bf16[2,112,3584]{2,1,0:T(8,128)(2,1)} %get-tuple-element.29) | copy-start | bytes 4816900

commit v5 on v4

--- a/solution.py
+++ b/solution.py
@@ -626,7 +626,7 @@
     total = SQ[0]
     for n in OTHERS:
         total += SQ[n]
-    sq_o[...] = total
+    sq_o[0, 0] = jnp.sum(total[:1, :1])
 
 
 def shape(dims, dtype=BF16):
@@ -667,9 +667,9 @@
     return pl.pallas_call(
         backward_kernel,
         name="backward",
-        out_shape=[shape((2, 112, FF)), shape((2, 112, FF)), shape((2, 448, D)), shape((8, 128), F32)],
+        out_shape=[shape((2, 112, FF)), shape((2, 112, FF)), shape((2, 448, D)), shape((1, 1), F32)],
         in_specs=[ANY] * 12,
-        out_specs=[ANY] * 3 + [pl.BlockSpec(memory_space=pltpu.VMEM)],
+        out_specs=[ANY] * 3 + [pl.BlockSpec(memory_space=pltpu.SMEM)],
         scratch_shapes=[
             pltpu.VMEM((TILES, 2, 8, 112, WIDE), BF16), pltpu.VMEM((4, 14, 64, D), BF16), pltpu.VMEM((T, D), BF16), pltpu.VMEM((2, 448, T), BF16),
             pltpu.VMEM((T, D), BF16), pltpu.VMEM((T, D), F32), *[pltpu.VMEM((T, WIDE), BF16)] * 3,
@@ -699,7 +699,7 @@
         gu, a0t, h1, a1, a1t, wd0, *ahead = forward(x[0], *shards)
         *gradients, squares = backward(a1, a1t, h1, dy[0], a0t, gu, wd0, *ahead, *shards)
         count = mesh.shape["s"] * sum(g.size for g in gradients)
-        factor = jnp.minimum(1.0, 0.5 * lax.rsqrt(squares[0, 0] / count + 1e-30))
+        factor = jnp.minimum(1.0, 0.5 * lax.rsqrt(squares.reshape(()) / count + 1e-30))
         new = [adamw(w.astype(F32), m, v, g.astype(F32) * factor) for w, m, v, g in zip(weights, m, v, gradients, strict=True)]
         return tuple(one[which] for which in range(3) for one in new)
 

time: 398 us -> 397 us (level)
  no operation moved by 1% of the time
where the time goes in v5:
time: 397 us; the launch traced here: 396 us
  Pallas kernels  375 us (94%)
  other arithmetic  14.8 us (4%)
  local copies, waits for them, and re-layouts  4.77 us (1%)
    pallas_call x1, Pallas kernels, backward(): pl.pallas_call(backward_kernel, name='backward', out_shape=[shape((2, 112...  279 us
    pallas_call x1, Pallas kernels, forward(): pl.pallas_call(forward_kernel, name='forward', out_shape=[shape((TILES, 2...  95.9 us
    convert_element_type x2, other arithmetic, adamw(): return ((w - 0.02 * step).astype(BF16), m, v)  14.8 us

profile of v5, /device:TPU:0, one launch (start us, length us, event | category | flops | bytes accessed | tf_op | source)
XLA Modules:
  0.0 396.3 jit_solution(8626977015004224212)
XLA Ops:
  0.6 95.9 %forward.1 = (f32[7,2,2048,512]{3,2,1,0:T(8,128)}, bf16[2,448,2048]{2,1,0:T(8,128)(2,1)}, bf16[2048,896]{1,0:T(8,128)(2,1)}, bf16[2048,896]{1,0:T(8,128)(2,1)}, ...) custom-call(bf16[2048,896]{1,0:T(8,128)(2,1)} %bitcast.6, ...), custom_call_target="tpu_custom_call" | custom-call | tf_op jit(solution)/shard_map/forward/pallas_call | solution.py:644
  96.5 279.4 %backward.1 = (bf16[2,112,3584]{2,1,0:T(8,128)(2,1)}, bf16[2,112,3584]{2,1,0:T(8,128)(2,1)}, bf16[2,448,896]{2,1,0:T(8,128)(2,1)}, f32[1,1]{1,0:T(1,128)}) custom-call(bf16[2048,896]{1,0:T(8,128)(2,1)} %get-tuple-element.21.a1_h, bf16[2,448,2048]{2,1,0:T(8,128)(2,1)} %get-tuple-element.22.a1t_h, bf16[2048,896]{1,0:T(8,128)(2,1)} %get-tuple-element.23.h1_h, ...), custom_call_target="tpu_custom_call" | custom-call | tf_op jit(solution)/shard_map/backward/pallas_call | solution.py:667
  376.7 0.0 copy-start
  376.7 0.0 copy-start.1
  376.7 0.0 copy-start.2
  376.7 0.0 copy-start.3
  376.8 0.0 copy-start.4
  376.8 0.0 copy-start.5
  376.8 0.0 copy-start.6
  376.8 6.9 %fusion.8 = (bf16[2,448,896]{2,1,0:T(8,128)(2,1)}, f32[2,448,896]{2,1,0:T(8,128)}, f32[2,448,896]{2,1,0:T(8,128)}) fusion(bf16[2,448,896]{2,1,0:T(8,128)(2,1)} %param.15, f32[]{:T(128)} %bitcast.3, bf16[2,448,896]{2,1,0:T(8,128)(2,1)} %get-tuple-element.32, f32[2,448,896]{2,1,0:T(8,128)} %param.21, f32[2,448,896]{2,1,0:T(8,128)} %param.18), kind=kLoop, calls=%fused_computation.17 | loop fusion | flops 13647872 | bytes 17661956 | tf_op jit(solution)/shard_map/convert_element_type | solution.py:692
  383.7 0.0 copy-done
  383.7 0.0 copy-done.1
  383.7 1.6 copy-done.2
  385.2 0.9 copy-done.3
  386.2 0.9 copy-done.4
  387.1 0.9 copy-done.5
  388.0 0.4 copy-done.6
  388.4 7.9 %fusion.2 = (bf16[2,112,3584]{2,1,0:T(8,128)(2,1)}, f32[2,112,3584]{2,1,0:T(8,128)}, f32[2,112,3584]{2,1,0:T(8,128)}, bf16[2,112,3584]{2,1,0:T(8,128)(2,1)}, f32...) fusion(bf16[2,112,3584]{2,1,0:T(8,128)(2,1)S(1)} %copy-done, f32[]{:T(128)} %bitcast.3, ...), kind=kLoop, calls=%fused_computation.11 | loop fusion | flops 27295744 | bytes 35323908 | tf_op jit(solution)/shard_map/convert_element_type | solution.py:692
Async XLA Ops:
  376.7 7.0 %copy-start = (bf16[2,112,3584]{2,1,0:T(8,128)(2,1)S(1)}, bf16[2,112,3584]{2,1,0:T(8,128)(2,1)}, u32[]{:S(2)}) copy-start(bf16[2,112,3584]{2,1,0:T(8,128)(2,1)} %wg_h.3) | copy-start | bytes 4816900
  376.7 7.0 %copy-start.1 = (bf16[2,112,3584]{2,1,0:T(8,128)(2,1)S(1)}, bf16[2,112,3584]{2,1,0:T(8,128)(2,1)}, u32[]{:S(2)}) copy-start(bf16[2,112,3584]{2,1,0:T(8,128)(2,1)} %wu_h.3) | copy-start | bytes 4816900
  376.7 8.5 %copy-start.2 = (f32[2,112,3584]{2,1,0:T(8,128)S(1)}, f32[2,112,3584]{2,1,0:T(8,128)}, u32[]{:S(2)}) copy-start(f32[2,112,3584]{2,1,0:T(8,128)} %param.19) | copy-start | bytes 9633796
  376.7 9.4 %copy-start.3 = (f32[2,112,3584]{2,1,0:T(8,128)S(1)}, f32[2,112,3584]{2,1,0:T(8,128)}, u32[]{:S(2)}) copy-start(f32[2,112,3584]{2,1,0:T(8,128)} %param.16) | copy-start | bytes 9633796
  376.8 10.3 %copy-start.4 = (f32[2,112,3584]{2,1,0:T(8,128)S(1)}, f32[2,112,3584]{2,1,0:T(8,128)}, u32[]{:S(2)}) copy-start(f32[2,112,3584]{2,1,0:T(8,128)} %param.20) | copy-start | bytes 9633796
  376.8 11.2 %copy-start.5 = (f32[2,112,3584]{2,1,0:T(8,128)S(1)}, f32[2,112,3584]{2,1,0:T(8,128)}, u32[]{:S(2)}) copy-start(f32[2,112,3584]{2,1,0:T(8,128)} %param.17) | copy-start | bytes 9633796
  376.8 11.7 %copy-start.6 = (bf16[2,112,3584]{2,1,0:T(8,128)(2,1)S(1)}, bf16[2,112,3584]{2,1,0:T(8,128)(2,1)}, u32[]{:S(2)}) copy-start(bf16[2,112,3584]{2,1,0:T(8,128)(2,1)} %get-tuple-element.29) | copy-start | bytes 4816900
